TPU v7x, 32 devices: a whole 2x2x4 slice. The times are simulated.
32 devices in a mesh: dp: 4 (over z), fsdp: 8 (over y, x, core).
Axes of the slice: x: 2, y: 2, z: 4, core: 2. Of those that a mesh axis runs over, the one named last changes fastest.
Arguments:
- emb_grad: float32 [4, 8, 2048, 4608], P('dp', 'fsdp')
- mat_grad: float32 [4, 8, 128, 4608], P('dp', 'fsdp')
- norm_grad: float32 [4, 8, 9, 4608], P('dp', 'fsdp')
- emb_param: float32 [2048, 4608], P('fsdp')
- emb_mom: float32 [2048, 4608], P('fsdp')
- emb_var: float32 [2048, 4608], P('fsdp')
- mat_param: float32 [128, 4608], P('fsdp')
- mat_mom: float32 [128, 4608], P('fsdp')
- mat_var: float32 [128, 4608], P('fsdp')
- norm_param: float32 [9, 4608], P(None, 'fsdp')
- norm_mom: float32 [9, 4608], P(None, 'fsdp')
- norm_var: float32 [9, 4608], P(None, 'fsdp')
Outputs:
- output 1: float32 [2048, 4608], P('fsdp')
- output 2: float32 [2048, 4608], P('fsdp')
- output 3: float32 [2048, 4608], P('fsdp')
- output 4: bfloat16 [2048, 4608], P('fsdp')
- output 5: float32 [128, 4608], P('fsdp')
- output 6: float32 [128, 4608], P('fsdp')
- output 7: float32 [128, 4608], P('fsdp')
- output 8: bfloat16 [128, 4608], P('fsdp')
- output 9: float32 [9, 4608], P(None, 'fsdp')
- output 10: float32 [9, 4608], P(None, 'fsdp')
- output 11: float32 [9, 4608], P(None, 'fsdp')
- output 12: bfloat16 [9, 4608], P(None, 'fsdp')
All inputs are finite; a program needn't handle non-finite values.
Results may differ from a plain program's by a relative error of at most 0.001.
Values sent between devices are 32-bit elements.
A program may use at most 1 GiB of HBM per device.

v0:
```python
import jax
import jax.numpy as jnp
from jax import lax
from jax.sharding import PartitionSpec as P

LEARN_RATE = 0.003
BETA_ONE = 0.9
BETA_TWO = 0.95
ADAM_EPS = 1e-8
WEIGHT_DECAY = 0.1
CLIP_NORM = 1.0
ADAM_STEP = 10


def adamw_update(grad_part, param_old, mom_old, var_old, decay_rate):
    new_mom = BETA_ONE * mom_old + (1.0 - BETA_ONE) * grad_part
    new_var = BETA_TWO * var_old + (1.0 - BETA_TWO) * grad_part * grad_part
    mom_hat = new_mom / (1.0 - BETA_ONE ** ADAM_STEP)
    var_hat = new_var / (1.0 - BETA_TWO ** ADAM_STEP)
    step_dir = mom_hat / (jnp.sqrt(var_hat) + ADAM_EPS)
    new_param = param_old - LEARN_RATE * (step_dir + decay_rate * param_old)
    return (new_param, new_mom, new_var, new_param.astype(jnp.bfloat16))


def solution(mesh):
    dev_count = mesh.shape["dp"] * mesh.shape["fsdp"]

    def local_step(emb_grad, mat_grad, norm_grad, emb_param, emb_mom, emb_var, mat_param, mat_mom, mat_var, norm_param, norm_mom, norm_var):
        emb_part = lax.psum_scatter(emb_grad[0, 0], "fsdp", scatter_dimension=0, tiled=True)
        mat_part = lax.psum_scatter(mat_grad[0, 0], "fsdp", scatter_dimension=0, tiled=True)
        norm_part = lax.psum_scatter(norm_grad[0, 0], "fsdp", scatter_dimension=1, tiled=True)
        emb_mean = lax.psum(emb_part, "dp") / dev_count
        mat_mean = lax.psum(mat_part, "dp") / dev_count
        norm_mean = lax.psum(norm_part, "dp") / dev_count
        local_sq = jnp.sum(emb_mean * emb_mean) + jnp.sum(mat_mean * mat_mean) + jnp.sum(norm_mean * norm_mean)
        total_sq = lax.psum(local_sq, "fsdp")
        clip_scale = jnp.minimum(1.0, CLIP_NORM / jnp.sqrt(total_sq))
        emb_out = adamw_update(emb_mean * clip_scale, emb_param, emb_mom, emb_var, WEIGHT_DECAY)
        mat_out = adamw_update(mat_mean * clip_scale, mat_param, mat_mom, mat_var, WEIGHT_DECAY)
        norm_out = adamw_update(norm_mean * clip_scale, norm_param, norm_mom, norm_var, 0.0)
        return emb_out + mat_out + norm_out

    grad_spec = P("dp", "fsdp", None, None)
    row_spec = P("fsdp", None)
    col_spec = P(None, "fsdp")
    in_list = (grad_spec, grad_spec, grad_spec, row_spec, row_spec, row_spec, row_spec, row_spec, row_spec, col_spec, col_spec, col_spec)
    out_list = (row_spec, row_spec, row_spec, row_spec, row_spec, row_spec, row_spec, row_spec, col_spec, col_spec, col_spec, col_spec)
    return jax.shard_map(local_step, mesh=mesh, in_specs=in_list, out_specs=out_list, check_vma=False)
```

profile of v0, /device:TPU:0, one launch (start us, length us, event | category | flops | bytes accessed | tf_op | source)
XLA Modules:
  0.0 557.1 jit_solution(2941479688521887470)
XLA Ops:
  7.2 0.0 reduce-scatter.8.cloned.1.call-start
  7.2 0.7 reduce-scatter.8.cloned.1.call-update
  7.9 0.0 reduce-scatter.6.cloned.1.call-start
  8.0 0.7 reduce-scatter.6.cloned.1.call-update
  8.7 0.0 reduce-scatter.10.cloned.1.call-start
  8.7 0.2 copy-done.4
  8.9 1.8 copy.26
  10.7 0.0 reduce-scatter.10.cloned.1.call-update
  10.7 0.0 all-reduce.3.cloned.1.call-start
  10.8 45.5 %reduce-scatter.8.cloned.1.call-done = f32[16,4608]{1,0:T(8,128)} async-done(((f32[128,4608]{1,0:T(8,128)}), f32[16,4608]{1,0:T(8,128)}) %reduce-scatter.8.cloned.1.call-update) | async-done | bytes 294928 | tf_op jit(solution)/shard_map/reduce_scatter | solution.py:30
  56.3 228.3 %reduce-scatter.6.cloned.1.call-done = f32[256,4608]{1,0:T(8,128)} async-done(((f32[2048,4608]{1,0:T(8,128)}), f32[256,4608]{1,0:T(8,128)}) %reduce-scatter.6.cloned.1.call-update) | async-done | bytes 4718608 | tf_op jit(solution)/shard_map/reduce_scatter | solution.py:29
  284.5 0.0 all-reduce.3.cloned.1.call-update
  284.6 46.1 %reduce-scatter.10.cloned.1.call-done = f32[576,9]{1,0:T(8,128)} async-done(((f32[4608,9]{1,0:T(8,128)}), f32[576,9]{1,0:T(8,128)}) %reduce-scatter.10.cloned.1.call-update) | async-done | bytes 20752
  330.6 1.1 copy.25
  331.7 20.4 %psum.30 = f32[9,576]{1,0:T(8,128)S(1)} all-reduce(f32[9,576]{1,0:T(8,128)S(1)} %copy.25), channel_id=1, replica_groups=mesh['dp'=4,'fsdp'=8] {'dp'}, use_global_device_ids=true, to_apply=%region_7.0 | all-reduce | flops 5184 | bytes 41472 | tf_op jit(solution)/shard_map/psum | solution.py:34
  352.2 0.6 multiply_reduce_fusion.2
  352.8 161.5 %all-reduce.3.cloned.1.call-done = (f32[256,4608]{1,0:T(8,128)}, f32[16,4608]{1,0:T(8,128)}) async-done(((f32[256,4608]{1,0:T(8,128)}, f32[16,4608]{1,0:T(8,128)}), (f32[256,4608]{1,0:T(8,128)}, f32[16,4608]{1,0:T(8,128)})) %all-reduce.3.cloned.1.call-update) | async-done | bytes 5013520 | tf_op jit(solution)/shard_map/psum | solution.py:32
  514.2 4.2 multiply_reduce_fusion
  518.4 0.7 multiply_reduce_fusion.1
  521.1 13.7 %psum.31 = f32[]{:T(128)} all-reduce(f32[]{:T(128)S(6)} %add.66), channel_id=1, replica_groups=mesh['dp'=4,'fsdp'=8] {'fsdp'}, use_global_device_ids=true, to_apply=%region_9.0 | all-reduce | flops 1 | bytes 8 | tf_op jit(solution)/shard_map/psum | solution.py:36
  535.5 0.0 copy-start.2
  535.6 13.2 %fusion.7 = (bf16[256,4608]{1,0:T(8,128)(2,1)}, f32[256,4608]{1,0:T(8,128)}, f32[256,4608]{1,0:T(8,128)}, f32[256,4608]{1,0:T(8,128)}) fusion(f32[256,4608]{1,0:T(8,128)} %param.15, f32[256,4608]{1,0:T(8,128)} %get-tuple-element.12, f32[]{:T(128)S(6)} %mul.139, f32[256,4608]{1,0:T(8,128)} %param.16, f32[256,4608]{1,0:T(8,128)} %param.17), kind=kLoop, calls=%fused_computation.17 | loop fusion | flops 20054016 | bytes 35389444 | tf_op jit(solution)/shard_map/convert_element_type | solution.py:22
  548.8 1.1 fusion.5
  549.9 0.7 fusion.3
  (14 shorter events, 0.0 us)
Async XLA Ops:
  7.2 49.1 %reduce-scatter.8.cloned.1.call-start = ((), (), s32[]{:S(2)}) async-start(), calls=%async_computation.4 | async-start | bytes 2654208 | tf_op jit(solution)/shard_map/reduce_scatter | solution.py:30
  7.9 276.6 %reduce-scatter.6.cloned.1.call-start = ((), (), s32[]{:S(2)}) async-start(), calls=%async_computation.3 | async-start | bytes 42467328 | tf_op jit(solution)/shard_map/reduce_scatter | solution.py:29
  8.0 0.9 copy-start.4
  8.7 322.0 %reduce-scatter.10.cloned.1.call-start = ((), (), s32[]{:S(2)}) async-start(), calls=%async_computation.5 | async-start | bytes 2654208
  10.7 503.5 %all-reduce.3.cloned.1.call-start = ((), (), s32[]{:S(2)}) async-start(), calls=%async_computation.6 | async-start | bytes 10027008 | tf_op jit(solution)/shard_map/psum | solution.py:32
  514.2 4.2 copy-start
  535.5 13.3 %copy-start.1 = (f32[16,4608]{1,0:T(8,128)S(1)}, f32[16,4608]{1,0:T(8,128)}, u32[]{:S(2)}) copy-start(f32[16,4608]{1,0:T(8,128)} %param.18) | copy-start | bytes 884740
  535.5 13.3 %copy-start.2 = (f32[16,4608]{1,0:T(8,128)S(1)}, f32[16,4608]{1,0:T(8,128)}, u32[]{:S(2)}) copy-start(f32[16,4608]{1,0:T(8,128)} %param.19) | copy-start | bytes 884740
  535.5 13.3 %copy-start.3 = (f32[16,4608]{1,0:T(8,128)S(1)}, f32[16,4608]{1,0:T(8,128)}, u32[]{:S(2)}) copy-start(f32[16,4608]{1,0:T(8,128)} %param.20) | copy-start | bytes 884740
  535.5 14.4 %copy-start.5 = (f32[9,576]{1,0:T(8,128)S(1)}, f32[9,576]{1,0:T(8,128)}, u32[]{:S(2)}) copy-start(f32[9,576]{1,0:T(8,128)} %param.21) | copy-start | bytes 62212
  535.5 14.4 %copy-start.6 = (f32[9,576]{1,0:T(8,128)S(1)}, f32[9,576]{1,0:T(8,128)}, u32[]{:S(2)}) copy-start(f32[9,576]{1,0:T(8,128)} %param.22) | copy-start | bytes 62212
  535.6 14.3 %copy-start.7 = (f32[9,576]{1,0:T(8,128)S(1)}, f32[9,576]{1,0:T(8,128)}, u32[]{:S(2)}) copy-start(f32[9,576]{1,0:T(8,128)} %param.23) | copy-start | bytes 62212
Sparse Core Ops, SparseCore 0:
  11.3 44.9 reduce-scatter.7
  59.9 224.5 reduce-scatter.5
  288.5 42.1 reduce-scatter.9
  332.9 181.2 all-reduce.2
where the time goes:
time: 557 us
  waiting for transfers between devices  483 us (87%)
  blocking collectives  34.2 us (6%)
  other arithmetic  20.5 us (4%)
  between operations  16.5 us (3%)
    reduce_scatter x1, waiting for transfers between devices, local_step(): lax.psum_scatter(emb_grad[0, 0], 'fsdp', scatter_dimension=0, tiled=True)  228 us
    psum x1, waiting for transfers between devices, local_step(): emb_mean = lax.psum(emb_part, 'dp') / dev_count  161 us
    unnamed x5, waiting for transfers between devices  47.5 us
    reduce_scatter x1, waiting for transfers between devices, local_step(): lax.psum_scatter(mat_grad[0, 0], 'fsdp', scatter_dimension=0, tiled=True)  45.5 us
    psum x1, blocking collectives, local_step(): norm_mean = lax.psum(norm_part, 'dp') / dev_count  20.4 us
    convert_element_type x3, other arithmetic, adamw_update(): return (new_param, new_mom, new_var, new_param.astype(jnp.bfloat16))  15 us
    psum x1, blocking collectives, local_step(): total_sq = lax.psum(local_sq, 'fsdp')  13.7 us
  transfers between devices with their start and end apart: 4, of which 4 were waited for; matrix products, arithmetic and copies ran while one was open for 1% of the time, Pallas kernels for 0%

commit v1 on v0

v1 whole, which is shorter than its diff:
```python
import functools

import jax
import jax.numpy as jnp
from jax import lax
from jax.experimental import pallas as pl
from jax.experimental.pallas import tpu as pltpu
from jax.sharding import PartitionSpec as P

LEARN_RATE = 0.003
BETA_ONE = 0.9
BETA_TWO = 0.95
ADAM_EPS = 1e-8
WEIGHT_DECAY = 0.1
CLIP_NORM = 1.0
ADAM_STEP = 10

MESH = pl.DeviceIdType.MESH
F32 = jnp.float32
LANES = 128
SPLIT = 2
AHEAD = 2
SLOTS = 4
LAG_ONE, LAG_TWO, LAG_SIDE, LAG_MID, LAG_BACK = 1, 2, 3, 4, 5
NORM_START, NORM_STEP = 2, 3


def adamw_update(grad_part, param_old, mom_old, var_old, decay_rate):
    new_mom = BETA_ONE * mom_old + (1.0 - BETA_ONE) * grad_part
    new_var = BETA_TWO * var_old + (1.0 - BETA_TWO) * grad_part * grad_part
    mom_hat = new_mom / (1.0 - BETA_ONE ** ADAM_STEP)
    var_hat = new_var / (1.0 - BETA_TWO ** ADAM_STEP)
    step_dir = mom_hat / (jnp.sqrt(var_hat) + ADAM_EPS)
    new_param = param_old - LEARN_RATE * (step_dir + decay_rate * param_old)
    return (new_param, new_mom, new_var, new_param.astype(jnp.bfloat16))


def reduce_kernel(inv_count, emb_ref, mat_ref, norm_ref, emb_out, mat_out, norm_out, sq_out,
                  acc, own, one, two, zin, zmid, norm_all, nsend, nown, nacc, none, ntwo, nzin, nzmid, sq_part, sq_all,
                  core_send, core_recv, own_sem, one_send, one_recv, two_send, two_recv,
                  side_send, side_recv, mid_send, mid_recv, back_send, emb_sem, mat_sem,
                  norm_sem, nsend_sem, nrecv_sem, sq_send, sq_recv):
    z = lax.axis_index("dp")
    f = lax.axis_index("fsdp")
    y, x, c = f // 4, (f // 2) % 2, f % 2
    width = acc.shape[4]
    cols = width // SPLIT
    rounds = acc.shape[3] // 8 * SPLIT
    is_end = (z == 0) | (z == 3)
    is_mid = (z == 1) | (z == 2)
    side = z + 1 - 2 * (z % 2)
    core_peer = (z, y * 4 + x * 2 + 1 - c)
    x_peer = (z, y * 4 + (1 - x) * 2 + c)
    y_peer = (z, (1 - y) * 4 + x * 2 + c)
    side_peer = (side, f)
    mid_peer = (lax.rem(3 - z, 4), f)

    def remote(src, dst, send_sem, recv_sem, peer):
        return pltpu.make_async_remote_copy(src, dst, send_sem, recv_sem, device_id=peer, device_id_type=MESH)

    def piece(q):
        return pl.ds(pl.multiple_of(lax.div(q, SPLIT) * 8, 8), 8), pl.ds(pl.multiple_of(lax.rem(q, SPLIT) * cols, LANES), cols)

    def load_own(q):
        slot = lax.rem(q, SLOTS)
        rb, cb = piece(q)

        @pl.when(q < rounds - SPLIT)
        def _():
            pltpu.make_async_copy(emb_ref.at[:, :, c, :, rb, cb], own.at[slot], own_sem.at[slot]).start()

        @pl.when(q >= rounds - SPLIT)
        def _():
            pltpu.make_async_copy(mat_ref.at[:, :, c, :, :, cb], own.at[slot], own_sem.at[slot]).start()

    norm_load = pltpu.make_async_copy(norm_ref, norm_all, norm_sem)
    norm_load.start()
    for q in range(AHEAD):
        load_own(jnp.int32(q))

    barrier = pltpu.get_barrier_semaphore()
    for step in range(1, 8):
        pl.semaphore_signal(barrier, inc=1, device_id=(z, lax.rem(f + step, 8)), device_id_type=MESH)
    pl.semaphore_signal(barrier, inc=1, device_id=side_peer, device_id_type=MESH)

    @pl.when(is_mid)
    def _():
        pl.semaphore_signal(barrier, inc=1, device_id=mid_peer, device_id_type=MESH)

        pl.semaphore_wait(barrier, 9)

    @pl.when(is_end)
    def _():
        pl.semaphore_wait(barrier, 8)

    def send_core(q, carry):
        rb, cb = piece(q)
        remote(emb_ref.at[:, :, 1 - c, :, rb, cb], acc.at[:, :, :, rb, cb], core_send, core_recv.at[q], core_peer).start()
        return carry

    lax.fori_loop(0, rounds - SPLIT, send_core, 0)
    for q in range(rounds - SPLIT, rounds):
        rb, cb = piece(jnp.int32(q))
        remote(mat_ref.at[:, :, 1 - c, :, :, cb], acc.at[:, :, :, rb, cb], core_send, core_recv.at[q], core_peer).start()

    norm_load.wait()
    shard = nacc.shape[3]
    for yy in range(2):
        for xx in range(2):
            first = norm_all[:, (4 * yy + 2 * xx) * shard:(4 * yy + 2 * xx + 1) * shard]
            second = norm_all[:, (4 * yy + 2 * xx + 1) * shard:(4 * yy + 2 * xx + 2) * shard]
            nsend[yy, xx] = jnp.where(c == 0, second, first)
            nown[yy, xx] = jnp.where(c == 0, first, second)
    sq_part[...] = jnp.zeros_like(sq_part)

    def one_copy(q, h):
        rb, cb = piece(q)
        if h == 0:
            return remote(acc.at[:, 1 - x, 0, rb, cb], one.at[0, :, rb, cb], one_send.at[0], one_recv.at[0, q], x_peer)
        return remote(acc.at[1 - y, :, 1, rb, cb], one.at[1, :, rb, cb], one_send.at[1], one_recv.at[1, q], y_peer)

    def two_copy(q, h):
        rb, cb = piece(q)
        if h == 0:
            return remote(acc.at[1 - y, x, 0, rb, cb], two.at[0, rb, cb], two_send.at[0], two_recv.at[0, q], y_peer)
        return remote(acc.at[y, 1 - x, 1, rb, cb], two.at[1, rb, cb], two_send.at[1], two_recv.at[1, q], x_peer)

    def side_copy(q):
        rb, cb = piece(q)
        return remote(acc.at[y, x, :, rb, cb], zin.at[:, rb, cb], side_send, side_recv.at[q], side_peer)

    def mid_copy(q):
        rb, cb = piece(q)
        return remote(acc.at[y, x, :, rb, cb], zmid.at[:, rb, cb], mid_send, mid_recv.at[q], mid_peer)

    def back_copy(q):
        rb, cb = piece(q)
        return remote(zin.at[:, rb, cb], zin.at[:, rb, cb], back_send, side_recv.at[q], side_peer)

    def store_out(q):
        rb, cb = piece(q)

        @pl.when(q < rounds - SPLIT)
        def _():
            pltpu.make_async_copy(zin.at[:, rb, cb], emb_out.at[:, rb, cb], emb_sem).start()

        @pl.when(q >= rounds - SPLIT)
        def _():
            pltpu.make_async_copy(zin.at[:, rb, cb], mat_out.at[:, :, cb], mat_sem).start()

    def add_squares(total):
        sq = total * total
        part = sq_part[...]
        for h in range(2):
            for j in range(cols // LANES):
                part = part + sq[h, :, j * LANES:(j + 1) * LANES]
        sq_part[...] = part

    def norm_core():
        return remote(nsend, nacc, nsend_sem.at[0], nrecv_sem.at[0], core_peer)

    def norm_one():
        return remote(nacc.at[:, 1 - x], none, nsend_sem.at[1], nrecv_sem.at[1], x_peer)

    def norm_two():
        return remote(nacc.at[1 - y, x], ntwo, nsend_sem.at[2], nrecv_sem.at[2], y_peer)

    def norm_side():
        return remote(nacc.at[y, x], nzin, nsend_sem.at[3], nrecv_sem.at[3], side_peer)

    def norm_mid():
        return remote(nacc.at[y, x], nzmid, nsend_sem.at[4], nrecv_sem.at[4], mid_peer)

    def norm_back():
        return remote(nzin, nzin, nsend_sem.at[5], nrecv_sem.at[3], side_peer)

    norm_core().start()

    def body(t, carry):
        @pl.when(t + AHEAD < rounds)
        def _():
            load_own(t + AHEAD)

        @pl.when(t < rounds)
        def _():
            rb, cb = piece(t)
            slot = lax.rem(t, SLOTS)
            pltpu.make_async_copy(own.at[slot], own.at[slot], own_sem.at[slot]).wait()
            pltpu.make_async_copy(own.at[slot], own.at[slot], core_recv.at[t]).wait()
            acc[:, :, :, rb, cb] = acc[:, :, :, rb, cb] + own[slot]
            one_copy(t, 0).start()
            one_copy(t, 1).start()

        q1 = t - LAG_ONE

        @pl.when((q1 >= 0) & (q1 < rounds))
        def _():
            rb, cb = piece(q1)
            one_copy(q1, 0).wait_recv()
            acc[:, x, 0, rb, cb] = acc[:, x, 0, rb, cb] + one[0, :, rb, cb]
            two_copy(q1, 0).start()
            one_copy(q1, 1).wait_recv()
            acc[y, :, 1, rb, cb] = acc[y, :, 1, rb, cb] + one[1, :, rb, cb]
            two_copy(q1, 1).start()

        q2 = t - LAG_TWO

        @pl.when((q2 >= 0) & (q2 < rounds))
        def _():
            rb, cb = piece(q2)
            two_copy(q2, 0).wait_recv()
            two_copy(q2, 1).wait_recv()
            acc[y, x, :, rb, cb] = acc[y, x, :, rb, cb] + two[:, rb, cb]

            @pl.when(is_end)
            def _():
                side_copy(q2).start()

        q3 = t - LAG_SIDE

        @pl.when(is_mid & (q3 >= 0) & (q3 < rounds))
        def _():
            rb, cb = piece(q3)
            side_copy(q3).wait_recv()
            acc[y, x, :, rb, cb] = acc[y, x, :, rb, cb] + zin[:, rb, cb]
            mid_copy(q3).start()

        q4 = t - LAG_MID

        @pl.when(is_mid & (q4 >= 0) & (q4 < rounds))
        def _():
            rb, cb = piece(q4)
            mid_copy(q4).wait_recv()
            total = (acc[y, x, :, rb, cb] + zmid[:, rb, cb]) * inv_count
            zin[:, rb, cb] = total
            back_copy(q4).start()
            store_out(q4)
            add_squares(total)

        q5 = t - LAG_BACK

        @pl.when(is_end & (q5 >= 0) & (q5 < rounds))
        def _():
            rb, cb = piece(q5)
            back_copy(q5).wait_recv()
            store_out(q5)
            add_squares(zin[:, rb, cb])

        @pl.when(t == NORM_START)
        def _():
            norm_core().wait_recv()
            nacc[...] = nacc[...] + nown[...]
            norm_one().start()

        @pl.when(t == NORM_START + NORM_STEP)
        def _():
            norm_one().wait_recv()
            nacc[:, x] = nacc[:, x] + none[...]
            norm_two().start()

        @pl.when(t == NORM_START + 2 * NORM_STEP)
        def _():
            norm_two().wait_recv()
            nacc[y, x] = nacc[y, x] + ntwo[...]

            @pl.when(is_end)
            def _():
                norm_side().start()

        @pl.when(is_mid & (t == NORM_START + 3 * NORM_STEP))
        def _():
            norm_side().wait_recv()
            nacc[y, x] = nacc[y, x] + nzin[...]
            norm_mid().start()

        @pl.when(is_mid & (t == NORM_START + 4 * NORM_STEP))
        def _():
            norm_mid().wait_recv()
            nzin[...] = (nacc[y, x] + nzmid[...]) * inv_count
            norm_back().start()

        @pl.when(is_end & (t == NORM_START + 5 * NORM_STEP))
        def _():
            norm_back().wait_recv()

        return carry

    lax.fori_loop(0, rounds + LAG_BACK, body, 0)

    norm_total = nzin[...]
    norm_out[...] = norm_total
    norm_sq = jnp.sum(norm_total * norm_total)
    corner = (lax.broadcasted_iota(jnp.int32, sq_part.shape, 0) == 0) & (lax.broadcasted_iota(jnp.int32, sq_part.shape, 1) == 0)
    sq_part[...] = sq_part[...] + jnp.where(corner, norm_sq, 0.0)

    for step in range(1, 8):
        remote(sq_part, sq_all.at[f], sq_send, sq_recv, (z, lax.rem(f + step, 8))).start()
    sq_all[f] = sq_part[...]
    seven = pltpu.make_async_copy(sq_all.at[pl.ds(0, 7)], sq_all.at[pl.ds(0, 7)], sq_recv)
    seven.wait()
    square = sq_all[0]
    for j in range(1, 8):
        square = square + sq_all[j]
    scale = jnp.minimum(1.0, CLIP_NORM / jnp.sqrt(jnp.broadcast_to(jnp.sum(square), square.shape)))
    sq_out[...] = scale

    pltpu.make_async_copy(sq_all.at[pl.ds(0, 7)], sq_all.at[pl.ds(0, 7)], sq_send).wait()
    pltpu.make_async_copy(acc, acc, core_send).wait()
    for h in range(2):
        pltpu.make_async_copy(one.at[h], one.at[h], one_send.at[h]).wait()
        pltpu.make_async_copy(two.at[h], two.at[h], two_send.at[h]).wait()
    norm_core().wait_send()
    norm_one().wait_send()
    norm_two().wait_send()
    pltpu.make_async_copy(emb_out, emb_out, emb_sem).wait()
    pltpu.make_async_copy(mat_out, mat_out, mat_sem).wait()

    @pl.when(is_end)
    def _():
        pltpu.make_async_copy(zin, zin, side_send).wait()
        norm_side().wait_send()

    @pl.when(is_mid)
    def _():
        pltpu.make_async_copy(zin, zin, mid_send).wait()
        pltpu.make_async_copy(zin, zin, back_send).wait()
        norm_mid().wait_send()
        norm_back().wait_send()


def solution(mesh):
    dev_count = mesh.shape["dp"] * mesh.shape["fsdp"]

    def local_step(emb_grad, mat_grad, norm_grad, emb_param, emb_mom, emb_var, mat_param, mat_mom, mat_var, norm_param, norm_mom, norm_var):
        width = emb_grad.shape[3]
        emb_half, mat_half = emb_param.shape[0] // 2, mat_param.shape[0] // 2
        count, shard = norm_param.shape
        emb_in = emb_grad.reshape(2, 2, 2, 2, emb_half, width)
        mat_in = mat_grad.reshape(2, 2, 2, 2, mat_half, width)
        norm_in = norm_grad.reshape(norm_grad.shape[2:])
        rows = emb_half + mat_half
        rounds = rows // 8 * SPLIT
        cols = width // SPLIT
        any_spec = pl.BlockSpec(memory_space=pl.ANY)
        vmem_spec = pl.BlockSpec(memory_space=pltpu.VMEM)
        dma = pltpu.SemaphoreType.DMA
        emb_mean, mat_mean, norm_mean, scale = pl.pallas_call(
            functools.partial(reduce_kernel, 1.0 / dev_count),
            out_shape=(
                jax.ShapeDtypeStruct((2, emb_half, width), F32),
                jax.ShapeDtypeStruct((2, mat_half, width), F32),
                jax.ShapeDtypeStruct((count, shard), F32),
                jax.ShapeDtypeStruct((8, LANES), F32),
            ),
            in_specs=[any_spec] * 3,
            out_specs=(any_spec, any_spec, vmem_spec, vmem_spec),
            scratch_shapes=[
                pltpu.VMEM((2, 2, 2, rows, width), F32),
                pltpu.VMEM((SLOTS, 2, 2, 2, 8, cols), F32),
                pltpu.VMEM((2, 2, rows, width), F32),
                pltpu.VMEM((2, rows, width), F32),
                pltpu.VMEM((2, rows, width), F32),
                pltpu.VMEM((2, rows, width), F32),
                pltpu.VMEM(norm_in.shape, F32),
                pltpu.VMEM((2, 2, count, shard), F32),
                pltpu.VMEM((2, 2, count, shard), F32),
                pltpu.VMEM((2, 2, count, shard), F32),
                pltpu.VMEM((2, count, shard), F32),
                pltpu.VMEM((count, shard), F32),
                pltpu.VMEM((count, shard), F32),
                pltpu.VMEM((count, shard), F32),
                pltpu.VMEM((8, LANES), F32),
                pltpu.VMEM((8, 8, LANES), F32),
                dma, dma((rounds,)), dma((SLOTS,)),
                dma((2,)), dma((2, rounds)), dma((2,)), dma((2, rounds)),
                dma, dma((rounds,)), dma, dma((rounds,)), dma,
                dma, dma,
                dma, dma((6,)), dma((6,)), dma, dma,
            ],
            compiler_params=pltpu.CompilerParams(collective_id=0, has_side_effects=True, vmem_limit_bytes=56 << 20),
            name="reduce_gradients",
        )(emb_in, mat_in, norm_in)
        clip_scale = scale[0, 0]
        emb_mean = emb_mean.reshape(emb_param.shape)
        mat_mean = mat_mean.reshape(mat_param.shape)
        emb_out = adamw_update(emb_mean * clip_scale, emb_param, emb_mom, emb_var, WEIGHT_DECAY)
        mat_out = adamw_update(mat_mean * clip_scale, mat_param, mat_mom, mat_var, WEIGHT_DECAY)
        norm_out = adamw_update(norm_mean * clip_scale, norm_param, norm_mom, norm_var, 0.0)
        return emb_out + mat_out + norm_out

    grad_spec = P("dp", "fsdp", None, None)
    row_spec = P("fsdp", None)
    col_spec = P(None, "fsdp")
    in_list = (grad_spec, grad_spec, grad_spec, row_spec, row_spec, row_spec, row_spec, row_spec, row_spec, col_spec, col_spec, col_spec)
    out_list = (row_spec, row_spec, row_spec, row_spec, row_spec, row_spec, row_spec, row_spec, col_spec, col_spec, col_spec, col_spec)
    return jax.shard_map(local_step, mesh=mesh, in_specs=in_list, out_specs=out_list, check_vma=False)
```

time: 557 us -> 231 us (0.41)
  waiting for transfers between devices: 483 us -> 0 us
  Pallas kernels: 0 us -> 211 us
  blocking collectives: 34.2 us -> 0 us
  between operations: 16.5 us -> 0.74 us
  other arithmetic: 20.5 us -> 14.2 us
    reduce_scatter x2 -> x0, waiting for transfers between devices: 274 us -> none  [the longest x1 228 us: local_step(): lax.psum_scatter(emb_grad[0, 0], 'fsdp', scatter_dimension=0, tiled=True)]
    pallas_call x0 -> x1, Pallas kernels: none -> 211 us  [local_step(): pl.pallas_call(functools.partial(reduce_kernel, 1.0 / dev_count), out_sha...]
    psum x1 -> x0, waiting for transfers between devices: 161 us -> none  [local_step(): emb_mean = lax.psum(emb_part, 'dp') / dev_count]
    unnamed x5 -> x0, waiting for transfers between devices: 47.5 us -> none
    psum x2 -> x0, blocking collectives: 34.2 us -> none  [the longest x1 20.4 us: local_step(): norm_mean = lax.psum(norm_part, 'dp') / dev_count]
  transfers between devices with their start and end apart: 4 -> 0, of which waited for: 4 -> 0; matrix products, arithmetic and copies ran while one was open for 1% -> 0% of each run, Pallas kernels for 0% -> 0%
where the time goes in v1:
time: 231 us; the launch traced here: 230 us
  Pallas kernels  211 us (91%)
  other arithmetic  14.2 us (6%)
  local copies, waits for them, and re-layouts  4.27 us (2%)
    pallas_call x1, Pallas kernels, local_step(): pl.pallas_call(functools.partial(reduce_kernel, 1.0 / dev_count), out_sha...  211 us
    convert_element_type x3, other arithmetic, adamw_update(): return (new_param, new_mom, new_var, new_param.astype(jnp.bfloat16))  10.4 us

profile of v1, /device:TPU:0, one launch (start us, length us, event | category | flops | bytes accessed | tf_op | source)
XLA Modules:
  0.0 230.3 jit_solution(17209934667342167908)
XLA Ops:
  0.6 1.7 copy.26
  2.3 0.0 copy-start.2
  2.3 211.1 %reduce_gradients.1 = (f32[2,128,4608]{2,1,0:T(8,128)}, f32[2,8,4608]{2,1,0:T(8,128)}, f32[9,576]{1,0:T(8,128)}, f32[8,128]{1,0:T(8,128)}) custom-call(f32[2,2,2,2,128,4608]{5,4,3,2,1,0:T(8,128)} %bitcast.20, f32[2,2,2,2,8,4608]{5,4,3,2,1,0:T(8,128)} %bitcast.21, f32[9,4608]{1,0:T(8,128)} %bitcast.22), custom_call_target="tpu_custom_call" | custom-call | tf_op jit(solution)/shard_map/reduce_gradients/pallas_call | solution.py:347
  213.4 1.2 slice.3
  214.6 0.0 copy-start
  214.6 3.8 %broadcast_multiply_fusion = f32[2,128,4608]{2,1,0:T(8,128)S(1)} fusion(f32[2,128,4608]{2,1,0:T(8,128)} %get-tuple-element.16, f32[]{:T(128)} %bitcast.2), kind=kLoop, calls=%fused_computation.5 | loop fusion | flops 1179648 | bytes 9437188 | tf_op jit(solution)/shard_map/mul | solution.py:386
  218.4 0.0 copy-done.2
  218.4 0.0 copy-done
  218.4 1.4 copy-done.1
  219.8 0.0 copy-start.7
  219.8 0.0 copy-start.8
  219.8 0.0 copy-start.9
  219.8 0.0 copy-start.10
  219.8 7.4 %fusion.10 = (bf16[256,4608]{1,0:T(8,128)(2,1)}, f32[256,4608]{1,0:T(8,128)}, f32[256,4608]{1,0:T(8,128)}, f32[256,4608]{1,0:T(8,128)}) fusion(f32[256,4608]{1,0:T(8,128)S(1)} %copy-done, f32[2,128,4608]{2,1,0:T(8,128)S(1)} %broadcast_multiply_fusion, f32[256,4608]{1,0:T(8,128)S(1)} %copy-done.1, f32[256,4608]{1,0:T(8,128)S(1)} %copy-done.2), kind=kLoop, calls=%fused_computation.18 | loop fusion | flops 18874368 | bytes 35389440 | tf_op jit(solution)/shard_map/convert_element_type | solution.py:35
  227.2 0.0 copy-done.3
  227.2 0.0 copy-done.4
  227.3 0.0 copy-done.5
  227.3 0.0 copy-done.6
  227.3 1.7 fusion.7
  229.0 0.0 copy-done.7
  229.0 0.0 copy-done.8
  229.0 0.0 copy-done.9
  229.0 0.0 copy-done.10
  229.0 1.3 fusion.5
  (5 shorter events, 0.0 us)
Async XLA Ops:
  2.3 216.1 %copy-start.2 = (f32[256,4608]{1,0:T(8,128)S(1)}, f32[256,4608]{1,0:T(8,128)}, u32[]{:S(2)}) copy-start(f32[256,4608]{1,0:T(8,128)} %param.17) | copy-start | bytes 14155780
  214.6 3.8 %copy-start = (f32[256,4608]{1,0:T(8,128)S(1)}, f32[256,4608]{1,0:T(8,128)}, u32[]{:S(2)}) copy-start(f32[256,4608]{1,0:T(8,128)} %param.15) | copy-start | bytes 14155780
  214.6 5.2 %copy-start.1 = (f32[256,4608]{1,0:T(8,128)S(1)}, f32[256,4608]{1,0:T(8,128)}, u32[]{:S(2)}) copy-start(f32[256,4608]{1,0:T(8,128)} %param.16) | copy-start | bytes 14155780
  219.8 7.5 %copy-start.3 = (f32[16,4608]{1,0:T(8,128)S(1)}, f32[16,4608]{1,0:T(8,128)}, u32[]{:S(2)}) copy-start(f32[16,4608]{1,0:T(8,128)} %param.18) | copy-start | bytes 884740
  219.8 7.5 %copy-start.4 = (f32[16,4608]{1,0:T(8,128)S(1)}, f32[16,4608]{1,0:T(8,128)}, u32[]{:S(2)}) copy-start(f32[16,4608]{1,0:T(8,128)} %param.19) | copy-start | bytes 884740
  219.8 7.5 %copy-start.5 = (f32[16,4608]{1,0:T(8,128)S(1)}, f32[16,4608]{1,0:T(8,128)}, u32[]{:S(2)}) copy-start(f32[16,4608]{1,0:T(8,128)} %param.20) | copy-start | bytes 884740
  219.8 7.5 %copy-start.6 = (f32[2,8,4608]{2,1,0:T(8,128)S(1)}, f32[2,8,4608]{2,1,0:T(8,128)}, u32[]{:S(2)}) copy-start(f32[2,8,4608]{2,1,0:T(8,128)} %get-tuple-element.18) | copy-start | bytes 884740
  219.8 9.2 %copy-start.7 = (f32[9,576]{1,0:T(8,128)S(1)}, f32[9,576]{1,0:T(8,128)}, u32[]{:S(2)}) copy-start(f32[9,576]{1,0:T(8,128)} %param.21) | copy-start | bytes 62212
  219.8 9.2 %copy-start.8 = (f32[9,576]{1,0:T(8,128)S(1)}, f32[9,576]{1,0:T(8,128)}, u32[]{:S(2)}) copy-start(f32[9,576]{1,0:T(8,128)} %param.22) | copy-start | bytes 62212
  219.8 9.2 %copy-start.9 = (f32[9,576]{1,0:T(8,128)S(1)}, f32[9,576]{1,0:T(8,128)}, u32[]{:S(2)}) copy-start(f32[9,576]{1,0:T(8,128)} %param.23) | copy-start | bytes 62212
  219.8 9.2 %copy-start.10 = (f32[9,576]{1,0:T(8,128)S(1)}, f32[9,576]{1,0:T(8,128)}, u32[]{:S(2)}) copy-start(f32[9,576]{1,0:T(8,128)} %get-tuple-element.19) | copy-start | bytes 62212

commit v2 on v1

--- a/solution.py
+++ b/solution.py
@@ -18,10 +18,11 @@
 MESH = pl.DeviceIdType.MESH
 F32 = jnp.float32
 LANES = 128
-SPLIT = 2
+SPLIT = 3
 AHEAD = 2
 SLOTS = 4
-LAG_ONE, LAG_TWO, LAG_SIDE, LAG_MID, LAG_BACK = 1, 2, 3, 4, 5
+CORE_AHEAD = 4
+LAG_ONE, LAG_TWO, LAG_SIDE, LAG_MID, LAG_BACK = 1, 2, 4, 6, 8
 NORM_START, NORM_STEP = 2, 3
 
 
@@ -93,15 +94,19 @@
     def _():
         pl.semaphore_wait(barrier, 8)
 
-    def send_core(q, carry):
-        rb, cb = piece(q)
-        remote(emb_ref.at[:, :, 1 - c, :, rb, cb], acc.at[:, :, :, rb, cb], core_send, core_recv.at[q], core_peer).start()
-        return carry
-
-    lax.fori_loop(0, rounds - SPLIT, send_core, 0)
-    for q in range(rounds - SPLIT, rounds):
-        rb, cb = piece(jnp.int32(q))
-        remote(mat_ref.at[:, :, 1 - c, :, :, cb], acc.at[:, :, :, rb, cb], core_send, core_recv.at[q], core_peer).start()
+    def send_core(q):
+        rb, cb = piece(q)
+
+        @pl.when(q < rounds - SPLIT)
+        def _():
+            remote(emb_ref.at[:, :, 1 - c, :, rb, cb], acc.at[:, :, :, rb, cb], core_send, core_recv.at[q], core_peer).start()
+
+        @pl.when(q >= rounds - SPLIT)
+        def _():
+            remote(mat_ref.at[:, :, 1 - c, :, :, cb], acc.at[:, :, :, rb, cb], core_send, core_recv.at[q], core_peer).start()
+
+    for q in range(CORE_AHEAD):
+        send_core(jnp.int32(q))
 
     norm_load.wait()
     shard = nacc.shape[3]
@@ -177,6 +182,10 @@
     norm_core().start()
 
     def body(t, carry):
+        @pl.when(t + CORE_AHEAD < rounds)
+        def _():
+            send_core(t + CORE_AHEAD)
+
         @pl.when(t + AHEAD < rounds)
         def _():
             load_own(t + AHEAD)

time: 231 us -> 212 us (0.918)
  Pallas kernels: 211 us -> 192 us
    pallas_call x1, Pallas kernels: 211 us -> 192 us  [local_step(): pl.pallas_call(functools.partial(reduce_kernel, 1.0 / dev_count), out_sha...]
where the time goes in v2:
time: 212 us; the launch traced here: 211 us
  Pallas kernels  192 us (91%)
  other arithmetic  14.2 us (7%)
  local copies, waits for them, and re-layouts  4.27 us (2%)
    pallas_call x1, Pallas kernels, local_step(): pl.pallas_call(functools.partial(reduce_kernel, 1.0 / dev_count), out_sha...  192 us
    convert_element_type x3, other arithmetic, adamw_update(): return (new_param, new_mom, new_var, new_param.astype(jnp.bfloat16))  10.4 us

profile of v2, /device:TPU:0, one launch (start us, length us, event | category | flops | bytes accessed | tf_op | source)
XLA Modules:
  0.0 211.5 jit_solution(12586068531435373161)
XLA Ops:
  0.6 1.7 copy.26
  2.3 0.0 copy-start.2
  2.3 192.2 %reduce_gradients.1 = (f32[2,128,4608]{2,1,0:T(8,128)}, f32[2,8,4608]{2,1,0:T(8,128)}, f32[9,576]{1,0:T(8,128)}, f32[8,128]{1,0:T(8,128)}) custom-call(f32[2,2,2,2,128,4608]{5,4,3,2,1,0:T(8,128)} %bitcast.20, f32[2,2,2,2,8,4608]{5,4,3,2,1,0:T(8,128)} %bitcast.21, f32[9,4608]{1,0:T(8,128)} %bitcast.22), custom_call_target="tpu_custom_call" | custom-call | tf_op jit(solution)/shard_map/reduce_gradients/pallas_call | solution.py:356
  194.6 1.2 slice.3
  195.8 0.0 copy-start
  195.8 3.8 %broadcast_multiply_fusion = f32[2,128,4608]{2,1,0:T(8,128)S(1)} fusion(f32[2,128,4608]{2,1,0:T(8,128)} %get-tuple-element.16, f32[]{:T(128)} %bitcast.2), kind=kLoop, calls=%fused_computation.5 | loop fusion | flops 1179648 | bytes 9437188 | tf_op jit(solution)/shard_map/mul | solution.py:395
  199.6 0.0 copy-done.2
  199.6 0.0 copy-done
  199.6 1.4 copy-done.1
  201.0 0.0 copy-start.7
  201.0 0.0 copy-start.8
  201.0 0.0 copy-start.9
  201.0 0.0 copy-start.10
  201.0 7.4 %fusion.10 = (bf16[256,4608]{1,0:T(8,128)(2,1)}, f32[256,4608]{1,0:T(8,128)}, f32[256,4608]{1,0:T(8,128)}, f32[256,4608]{1,0:T(8,128)}) fusion(f32[256,4608]{1,0:T(8,128)S(1)} %copy-done, f32[2,128,4608]{2,1,0:T(8,128)S(1)} %broadcast_multiply_fusion, f32[256,4608]{1,0:T(8,128)S(1)} %copy-done.1, f32[256,4608]{1,0:T(8,128)S(1)} %copy-done.2), kind=kLoop, calls=%fused_computation.18 | loop fusion | flops 18874368 | bytes 35389440 | tf_op jit(solution)/shard_map/convert_element_type | solution.py:36
  208.4 0.0 copy-done.3
  208.4 0.0 copy-done.4
  208.4 0.0 copy-done.5
  208.4 0.0 copy-done.6
  208.5 1.7 fusion.7
  210.2 0.0 copy-done.7
  210.2 0.0 copy-done.8
  210.2 0.0 copy-done.9
  210.2 0.0 copy-done.10
  210.2 1.3 fusion.5
  (5 shorter events, 0.0 us)
Async XLA Ops:
  2.3 197.3 %copy-start.2 = (f32[256,4608]{1,0:T(8,128)S(1)}, f32[256,4608]{1,0:T(8,128)}, u32[]{:S(2)}) copy-start(f32[256,4608]{1,0:T(8,128)} %param.17) | copy-start | bytes 14155780
  195.8 3.8 %copy-start = (f32[256,4608]{1,0:T(8,128)S(1)}, f32[256,4608]{1,0:T(8,128)}, u32[]{:S(2)}) copy-start(f32[256,4608]{1,0:T(8,128)} %param.15) | copy-start | bytes 14155780
  195.8 5.2 %copy-start.1 = (f32[256,4608]{1,0:T(8,128)S(1)}, f32[256,4608]{1,0:T(8,128)}, u32[]{:S(2)}) copy-start(f32[256,4608]{1,0:T(8,128)} %param.16) | copy-start | bytes 14155780
  200.9 7.5 %copy-start.3 = (f32[16,4608]{1,0:T(8,128)S(1)}, f32[16,4608]{1,0:T(8,128)}, u32[]{:S(2)}) copy-start(f32[16,4608]{1,0:T(8,128)} %param.18) | copy-start | bytes 884740
  201.0 7.5 %copy-start.4 = (f32[16,4608]{1,0:T(8,128)S(1)}, f32[16,4608]{1,0:T(8,128)}, u32[]{:S(2)}) copy-start(f32[16,4608]{1,0:T(8,128)} %param.19) | copy-start | bytes 884740
  201.0 7.5 %copy-start.5 = (f32[16,4608]{1,0:T(8,128)S(1)}, f32[16,4608]{1,0:T(8,128)}, u32[]{:S(2)}) copy-start(f32[16,4608]{1,0:T(8,128)} %param.20) | copy-start | bytes 884740
  201.0 7.5 %copy-start.6 = (f32[2,8,4608]{2,1,0:T(8,128)S(1)}, f32[2,8,4608]{2,1,0:T(8,128)}, u32[]{:S(2)}) copy-start(f32[2,8,4608]{2,1,0:T(8,128)} %get-tuple-element.18) | copy-start | bytes 884740
  201.0 9.2 %copy-start.7 = (f32[9,576]{1,0:T(8,128)S(1)}, f32[9,576]{1,0:T(8,128)}, u32[]{:S(2)}) copy-start(f32[9,576]{1,0:T(8,128)} %param.21) | copy-start | bytes 62212
  201.0 9.2 %copy-start.8 = (f32[9,576]{1,0:T(8,128)S(1)}, f32[9,576]{1,0:T(8,128)}, u32[]{:S(2)}) copy-start(f32[9,576]{1,0:T(8,128)} %param.22) | copy-start | bytes 62212
  201.0 9.2 %copy-start.9 = (f32[9,576]{1,0:T(8,128)S(1)}, f32[9,576]{1,0:T(8,128)}, u32[]{:S(2)}) copy-start(f32[9,576]{1,0:T(8,128)} %param.23) | copy-start | bytes 62212
  201.0 9.2 %copy-start.10 = (f32[9,576]{1,0:T(8,128)S(1)}, f32[9,576]{1,0:T(8,128)}, u32[]{:S(2)}) copy-start(f32[9,576]{1,0:T(8,128)} %get-tuple-element.19) | copy-start | bytes 62212

commit v3 on v0

v3 whole, which is shorter than its diff:
```python
import functools

import jax
import jax.numpy as jnp
from jax import lax
from jax.experimental import pallas as pl
from jax.experimental.pallas import tpu as pltpu
from jax.sharding import PartitionSpec as P

LEARN_RATE = 0.003
BETA_ONE = 0.9
BETA_TWO = 0.95
ADAM_EPS = 1e-8
WEIGHT_DECAY = 0.1
CLIP_NORM = 1.0
ADAM_STEP = 10

MESH = pl.DeviceIdType.MESH
F32 = jnp.float32
LANES = 128
SPLIT = 2
AHEAD = 2
SLOTS = 4
CORE_AHEAD = 4
LAG_ONE, LAG_TWO, LAG_SIDE, LAG_MID, LAG_BACK = 2, 4, 6, 8, 10
NORM_START, NORM_STEP = 4, 6
LINE_BLOCKS = 4
LINE_SPLIT = 3
LINE_RATE, LINE_STEP = 4, 2
ADAM_ROWS = 32
VMEM_MIB = 52


def reduce_kernel(inv_count, emb_ref, mat_ref, norm_ref, emb_out, mat_out, norm_out, scale_out,
                  acc, own, one, two, zin, zmid, lown, lside, lmid, lback, lone, ltwo,
                  norm_all, nsend, nown, nacc, none, ntwo, nzin, nzmid, sq_main, sq_line, sq_all,
                  core_send, core_recv, own_sem, one_send, one_recv, two_send, two_recv,
                  side_send, side_recv, mid_send, mid_recv, back_send, emb_sem, mat_sem,
                  lown_sem, line_send, line_recv, norm_sem, nsend_sem, nrecv_sem, sq_send, sq_recv):
    z = lax.axis_index("dp")
    f = lax.axis_index("fsdp")
    y, x, c = f // 4, (f // 2) % 2, f % 2
    width = acc.shape[3]
    half = width // 2
    cols = half // SPLIT
    emb_blocks = emb_ref.shape[3] // 8
    rounds = one.shape[2] // 8 * SPLIT
    emb_rounds = (emb_blocks - LINE_BLOCKS) * SPLIT
    lines = lown.shape[0]
    lwidth = width // LINE_SPLIT
    quarter = lwidth // 4
    is_end = (z == 0) | (z == 3)
    is_mid = (z == 1) | (z == 2)
    high = z // 2
    side = z + 1 - 2 * (z % 2)
    core_peer = (z, y * 4 + x * 2 + 1 - c)
    x_peer = (z, y * 4 + (1 - x) * 2 + c)
    y_peer = (z, (1 - y) * 4 + x * 2 + c)
    side_peer = (side, f)
    mid_peer = (lax.rem(3 - z, 4), f)

    def remote(src, dst, send_sem, recv_sem, peer):
        return pltpu.make_async_remote_copy(src, dst, send_sem, recv_sem, device_id=peer, device_id_type=MESH)

    def take(ref, sem):
        pltpu.make_async_copy(ref, ref, sem).wait()

    def piece(q):
        block, sub = lax.div(q, SPLIT), lax.rem(q, SPLIT) * cols
        rows = pl.ds(pl.multiple_of((block + LINE_BLOCKS) * 8, 8), 8)
        inner = pl.ds(pl.multiple_of(block * 8, 8), 8)
        wide = [pl.ds(pl.multiple_of(sub + h * half, LANES), cols) for h in range(2)]
        return rows, inner, wide, pl.ds(pl.multiple_of(sub, LANES), cols)

    def mat_rows(q):
        return pl.ds(pl.multiple_of((lax.div(q, SPLIT) + LINE_BLOCKS - emb_blocks) * 8, 8), 8)

    def from_emb_or_mat(q, do):
        rows, _, wide, _ = piece(q)

        @pl.when(q < emb_rounds)
        def _():
            for h in range(2):
                do(emb_ref, rows, h, wide[h])

        @pl.when(q >= emb_rounds)
        def _():
            for h in range(2):
                do(mat_ref, mat_rows(q), h, wide[h])

    def load_own(q):
        slot = lax.rem(q, SLOTS)
        from_emb_or_mat(q, lambda ref, rows, h, cs: pltpu.make_async_copy(
            ref.at[:, :, c, rows, cs], own.at[slot, h], own_sem.at[slot]).start())

    def send_core(q):
        rb = piece(q)[0]
        from_emb_or_mat(q, lambda ref, rows, h, cs: remote(
            ref.at[:, :, 1 - c, rows, cs], acc.at[:, :, rb, cs], core_send, core_recv.at[q], core_peer).start())

    def line_at(i, start=0, size=4):
        rows = pl.ds(pl.multiple_of(lax.div(i, LINE_SPLIT) * 8, 8), 8)
        return rows, pl.ds(pl.multiple_of(lax.rem(i, LINE_SPLIT) * lwidth + start * quarter, LANES), size * quarter)

    def load_line(i):
        rows, cs = line_at(i)
        return pltpu.make_async_copy(emb_ref.at[:, :, c, rows, cs], lown.at[i], lown_sem.at[i])

    def line_core(i):
        rows, cs = line_at(i)
        return remote(emb_ref.at[:, :, 1 - c, rows, cs], acc.at[:, :, rows, cs], line_send.at[0], line_recv.at[0, i], core_peer)

    norm_load = pltpu.make_async_copy(norm_ref, norm_all, norm_sem)
    norm_load.start()
    for q in range(AHEAD):
        load_own(jnp.int32(q))
    for i in range(lines):
        load_line(jnp.int32(i)).start()

    barrier = pltpu.get_barrier_semaphore()
    for step in range(1, 8):
        pl.semaphore_signal(barrier, inc=1, device_id=(z, lax.rem(f + step, 8)), device_id_type=MESH)
    pl.semaphore_signal(barrier, inc=1, device_id=side_peer, device_id_type=MESH)

    @pl.when(is_mid)
    def _():
        pl.semaphore_signal(barrier, inc=1, device_id=mid_peer, device_id_type=MESH)
        pl.semaphore_wait(barrier, 9)

    @pl.when(is_end)
    def _():
        pl.semaphore_wait(barrier, 8)

    for q in range(CORE_AHEAD):
        if q % LINE_RATE == 0:
            line_core(jnp.int32(q // LINE_RATE)).start()
        send_core(jnp.int32(q))

    norm_load.wait()
    shard = nacc.shape[4]
    for yy in range(2):
        for xx in range(2):
            at = (4 * yy + 2 * xx) * shard
            first = norm_all[:, :, at:at + shard]
            second = norm_all[:, :, at + shard:at + 2 * shard]
            nsend[yy, xx] = jnp.where(c == 0, second, first)
            nown[yy, xx] = jnp.where(c == 0, first, second)
    sq_main[...] = jnp.zeros_like(sq_main)
    sq_line[...] = jnp.zeros_like(sq_line)

    def one_copy(q, h):
        rb, inner, wide, cs = piece(q)
        src = acc.at[:, 1 - x, rb, wide[0]] if h == 0 else acc.at[1 - y, :, rb, wide[1]]
        return remote(src, one.at[h, :, inner, cs], one_send.at[h], one_recv.at[h, q], (x_peer, y_peer)[h])

    def two_copy(q, h):
        rb, inner, wide, cs = piece(q)
        src = acc.at[1 - y, x, rb, wide[0]] if h == 0 else acc.at[y, 1 - x, rb, wide[1]]
        return remote(src, two.at[h, inner, cs], two_send.at[h], two_recv.at[h, q], (y_peer, x_peer)[h])

    def side_start(q):
        rb, _, wide, _ = piece(q)
        for cs in wide:
            remote(acc.at[y, x, rb, cs], zin.at[rb, cs], side_send, side_recv.at[q], side_peer).start()

    def mid_start(q):
        rb, inner, wide, _ = piece(q)
        for cs in wide:
            remote(acc.at[y, x, rb, cs], zmid.at[inner, cs], mid_send, mid_recv.at[q], mid_peer).start()

    def back_start(q):
        rb, _, wide, _ = piece(q)
        for cs in wide:
            remote(zin.at[rb, cs], zin.at[rb, cs], back_send, side_recv.at[q], side_peer).start()

    def both(q):
        _, inner, _, cs = piece(q)
        return two.at[:, inner, cs]

    def store_out(q):
        rb, _, wide, _ = piece(q)

        @pl.when(q < emb_rounds)
        def _():
            for cs in wide:
                pltpu.make_async_copy(zin.at[rb, cs], emb_out.at[rb, cs], emb_sem).start()

        @pl.when(q >= emb_rounds)
        def _():
            for cs in wide:
                pltpu.make_async_copy(zin.at[rb, cs], mat_out.at[mat_rows(q), cs], mat_sem).start()

    def add_squares(part_ref, total):
        sq = total * total
        part = part_ref[...]
        for j in range(total.shape[1] // LANES):
            part = part + sq[:, j * LANES:(j + 1) * LANES]
        part_ref[...] = part

    def line_side(i):
        rows, cs = line_at(i, 1 - high, 3)
        return remote(acc.at[:, :, rows, cs], lside.at[i], line_send.at[1], line_recv.at[1, i], side_peer)

    def line_mid(i):
        rows, cs = line_at(i, 2 - 2 * high, 2)
        return remote(acc.at[:, :, rows, cs], lmid.at[i], line_send.at[2], line_recv.at[2, i], mid_peer)

    def line_back(i):
        rows, cs = line_at(i, 3 * high, 1)
        return remote(acc.at[:, :, rows, cs], lback.at[i], line_send.at[3], line_recv.at[3, i], side_peer)

    def line_one(i, h):
        rows, cs = line_at(i, z, 1)
        src = acc.at[:, 1 - x, rows, cs] if h == 0 else acc.at[1 - y, :, rows, cs]
        return remote(src, lone.at[i], line_send.at[4], line_recv.at[4, i], (x_peer, y_peer)[h])

    def line_two(i, h):
        rows, cs = line_at(i, z, 1)
        src = acc.at[1 - y, x, rows, cs] if h == 0 else acc.at[y, 1 - x, rows, cs]
        return remote(src, ltwo.at[i], line_send.at[5], line_recv.at[5, i], (y_peer, x_peer)[h])

    def gather_side(i):
        rows, cs = line_at(i, 3 * high, 1)
        return remote(zin.at[rows, cs], zin.at[rows, cs], line_send.at[6], line_recv.at[6, i], side_peer)

    def gather_mid(i):
        rows, cs = line_at(i, 2 * high, 2)
        return remote(zin.at[rows, cs], zin.at[rows, cs], line_send.at[7], line_recv.at[7, i], mid_peer)

    def gather_back(i):
        rows, cs = line_at(i, 1 - high, 3)
        return remote(zin.at[rows, cs], zin.at[rows, cs], line_send.at[8], line_recv.at[8, i], side_peer)

    def line_out(i):
        rows, cs = line_at(i)
        pltpu.make_async_copy(zin.at[rows, cs], emb_out.at[rows, cs], emb_sem).start()
        add_squares(sq_line, zin[rows, cs])

    def either_way(i, do):
        @pl.when(lax.rem(i, 2) == 0)
        def _():
            do(0)

        @pl.when(lax.rem(i, 2) == 1)
        def _():
            do(1)

    def line_stage_0(i):
        rows, cs = line_at(i)
        load_line(i).wait()
        take(lown.at[i], line_recv.at[0, i])
        acc[:, :, rows, cs] = acc[:, :, rows, cs] + lown[i]

        @pl.when(is_end)
        def _():
            line_side(i).start()

    def line_stage_1(i):
        @pl.when(is_mid)
        def _():
            rows, cs = line_at(i, 1 - high, 3)
            take(lside.at[i], line_recv.at[1, i])
            acc[:, :, rows, cs] = acc[:, :, rows, cs] + lside[i]
            line_mid(i).start()

    def line_stage_2(i):
        @pl.when(is_mid)
        def _():
            rows, cs = line_at(i, 2 * high, 2)
            take(lmid.at[i], line_recv.at[2, i])
            acc[:, :, rows, cs] = acc[:, :, rows, cs] + lmid[i]
            line_back(i).start()

    def line_stage_3(i):
        @pl.when(is_end)
        def _():
            rows, cs = line_at(i, 3 * high, 1)
            take(lback.at[i], line_recv.at[3, i])
            acc[:, :, rows, cs] = acc[:, :, rows, cs] + lback[i]

        either_way(i, lambda h: line_one(i, h).start())

    def line_stage_4(i):
        rows, cs = line_at(i, z, 1)
        take(lone.at[i], line_recv.at[4, i])

        def add(h):
            if h == 0:
                acc[:, x, rows, cs] = acc[:, x, rows, cs] + lone[i]
            else:
                acc[y, :, rows, cs] = acc[y, :, rows, cs] + lone[i]
            line_two(i, h).start()

        either_way(i, add)

    def line_stage_5(i):
        rows, cs = line_at(i, z, 1)
        take(ltwo.at[i], line_recv.at[5, i])
        zin[rows, cs] = (acc[y, x, rows, cs] + ltwo[i]) * inv_count

        @pl.when(is_end)
        def _():
            gather_side(i).start()

    def line_stage_6(i):
        @pl.when(is_mid)
        def _():
            take(ltwo.at[i], line_recv.at[6, i])
            gather_mid(i).start()

    def line_stage_7(i):
        @pl.when(is_mid)
        def _():
            take(lone.at[i], line_recv.at[7, i])
            gather_back(i).start()
            line_out(i)

    def line_stage_8(i):
        @pl.when(is_end)
        def _():
            take(lside.at[i, 0, 0], line_recv.at[8, i])
            line_out(i)

    line_stages = (line_stage_0, line_stage_1, line_stage_2, line_stage_3, line_stage_4, line_stage_5, line_stage_6,
                   line_stage_7, line_stage_8)

    norm_core = remote(nsend, nacc, nsend_sem.at[0], nrecv_sem.at[0], core_peer)
    norm_one = remote(nacc.at[:, 1 - x], none, nsend_sem.at[1], nrecv_sem.at[1], x_peer)
    norm_two = remote(nacc.at[1 - y, x], ntwo, nsend_sem.at[2], nrecv_sem.at[2], y_peer)
    norm_side = remote(nacc.at[y, x], nzin, nsend_sem.at[3], nrecv_sem.at[3], side_peer)
    norm_mid = remote(nacc.at[y, x], nzmid, nsend_sem.at[4], nrecv_sem.at[4], mid_peer)
    norm_back = remote(nzin, nzin, nsend_sem.at[5], nrecv_sem.at[3], side_peer)
    norm_core.start()

    def body(t, carry):
        @pl.when(t + CORE_AHEAD < rounds)
        def _():
            send_core(t + CORE_AHEAD)

        @pl.when(t + AHEAD < rounds)
        def _():
            load_own(t + AHEAD)

        early = t + CORE_AHEAD

        @pl.when((lax.rem(early, LINE_RATE) == 0) & (early < lines * LINE_RATE))
        def _():
            line_core(lax.div(early, LINE_RATE)).start()

        @pl.when(t < rounds)
        def _():
            rb, _, wide, _ = piece(t)
            slot = lax.rem(t, SLOTS)
            take(own.at[slot], own_sem.at[slot])
            take(own.at[slot], core_recv.at[t])
            for h in range(2):
                acc[:, :, rb, wide[h]] = acc[:, :, rb, wide[h]] + own[slot, h]
                one_copy(t, h).start()

        q1 = t - LAG_ONE

        @pl.when((q1 >= 0) & (q1 < rounds))
        def _():
            rb, inner, wide, cs = piece(q1)
            one_copy(q1, 0).wait_recv()
            acc[:, x, rb, wide[0]] = acc[:, x, rb, wide[0]] + one[0, :, inner, cs]
            two_copy(q1, 0).start()
            one_copy(q1, 1).wait_recv()
            acc[y, :, rb, wide[1]] = acc[y, :, rb, wide[1]] + one[1, :, inner, cs]
            two_copy(q1, 1).start()

        q2 = t - LAG_TWO

        @pl.when((q2 >= 0) & (q2 < rounds))
        def _():
            rb, inner, wide, cs = piece(q2)
            for h in range(2):
                two_copy(q2, h).wait_recv()
                acc[y, x, rb, wide[h]] = acc[y, x, rb, wide[h]] + two[h, inner, cs]

            @pl.when(is_end)
            def _():
                side_start(q2)

        q3 = t - LAG_SIDE

        @pl.when(is_mid & (q3 >= 0) & (q3 < rounds))
        def _():
            rb, _, wide, _ = piece(q3)
            take(both(q3), side_recv.at[q3])
            for cs in wide:
                acc[y, x, rb, cs] = acc[y, x, rb, cs] + zin[rb, cs]
            mid_start(q3)

        q4 = t - LAG_MID

        @pl.when(is_mid & (q4 >= 0) & (q4 < rounds))
        def _():
            rb, inner, wide, _ = piece(q4)
            take(both(q4), mid_recv.at[q4])
            for cs in wide:
                total = (acc[y, x, rb, cs] + zmid[inner, cs]) * inv_count
                zin[rb, cs] = total
                add_squares(sq_main, total)
            back_start(q4)
            store_out(q4)

        q5 = t - LAG_BACK

        @pl.when(is_end & (q5 >= 0) & (q5 < rounds))
        def _():
            rb, _, wide, _ = piece(q5)
            take(both(q5), side_recv.at[q5])
            store_out(q5)
            for cs in wide:
                add_squares(sq_main, zin[rb, cs])

        for k, stage in enumerate(line_stages):
            late = t - k * LINE_STEP

            @pl.when((late >= 0) & (late < lines * LINE_RATE) & (lax.rem(late, LINE_RATE) == 0))
            def _(late=late, stage=stage):
                stage(lax.div(late, LINE_RATE))

        @pl.when(t == NORM_START)
        def _():
            norm_core.wait_recv()
            nacc[...] = nacc[...] + nown[...]
            norm_one.start()

        @pl.when(t == NORM_START + NORM_STEP)
        def _():
            norm_one.wait_recv()
            nacc[:, x] = nacc[:, x] + none[...]
            norm_two.start()

        @pl.when(t == NORM_START + 2 * NORM_STEP)
        def _():
            norm_two.wait_recv()
            nacc[y, x] = nacc[y, x] + ntwo[...]

            @pl.when(is_end)
            def _():
                norm_side.start()

        @pl.when(is_mid & (t == NORM_START + 3 * NORM_STEP))
        def _():
            norm_side.wait_recv()
            nacc[y, x] = nacc[y, x] + nzin[...]
            norm_mid.start()

        @pl.when(is_mid & (t == NORM_START + 4 * NORM_STEP))
        def _():
            norm_mid.wait_recv()
            nzin[...] = (nacc[y, x] + nzmid[...]) * inv_count
            norm_back.start()

        @pl.when(is_end & (t == NORM_START + 5 * NORM_STEP))
        def _():
            norm_back.wait_recv()

        @pl.when(t == NORM_START + 6 * NORM_STEP)
        def _():
            for j in range(norm_out.shape[0]):
                norm_out[j:j + 1, :] = nzin[j]
            norm_total = nzin[...]
            norm_sq = jnp.sum(norm_total * norm_total)
            corner = [lax.broadcasted_iota(jnp.int32, sq_line.shape, d) == 0 for d in range(2)]
            sq_norm = jnp.where(corner[0] & corner[1], norm_sq, 0.0)
            sq_all[0] = sq_norm

        return carry

    lax.fori_loop(0, rounds + LAG_BACK, body, 0)

    sq_main[...] = sq_main[...] + sq_line[...] + sq_all[0]
    for step in range(1, 8):
        remote(sq_main, sq_all.at[1 + f], sq_send, sq_recv, (z, lax.rem(f + step, 8))).start()
    sq_all[1 + f] = sq_main[...]
    seven = sq_all.at[pl.ds(0, 7)]
    take(seven, sq_recv)
    square = sq_all[1]
    for j in range(2, 9):
        square = square + sq_all[j]
    scale_out[...] = jnp.minimum(1.0, CLIP_NORM / jnp.sqrt(jnp.broadcast_to(jnp.sum(square), square.shape)))

    take(seven, sq_send)
    take(acc.at[:, :, pl.ds(0, one.shape[2])], core_send)
    for h in range(2):
        take(one.at[h], one_send.at[h])
        take(two.at[h], two_send.at[h])
    take(lown, line_send.at[0])
    take(lone, line_send.at[4])
    take(ltwo, line_send.at[5])
    norm_core.wait_send()
    norm_one.wait_send()
    norm_two.wait_send()
    take(emb_out, emb_sem)
    take(mat_out, mat_sem)

    @pl.when(is_end)
    def _():
        take(zmid, side_send)
        take(lside, line_send.at[1])
        take(ltwo, line_send.at[6])
        norm_side.wait_send()

    @pl.when(is_mid)
    def _():
        take(zmid, mid_send)
        take(zmid, back_send)
        take(lmid, line_send.at[2])
        take(lback, line_send.at[3])
        take(lone, line_send.at[7])
        take(lside.at[:, 0, 0], line_send.at[8])
        norm_mid.wait_send()
        norm_back.wait_send()


def adam_kernel(scale_ref, *refs):
    ins, outs = refs[:12], refs[12:]
    clip = scale_ref[0:1, 0:1]
    bias_one = 1.0 / (1.0 - BETA_ONE ** ADAM_STEP)
    bias_two = 1.0 / (1.0 - BETA_TWO ** ADAM_STEP)

    def update(group, rows, decay_rate):
        grad, param, mom, var = (ref[rows, :] for ref in ins[4 * group:4 * group + 4])
        grad = grad * clip
        new_mom = BETA_ONE * mom + (1.0 - BETA_ONE) * grad
        new_var = BETA_TWO * var + (1.0 - BETA_TWO) * grad * grad
        step_dir = new_mom * bias_one / (jnp.sqrt(new_var * bias_two) + ADAM_EPS)
        new_param = param - LEARN_RATE * (step_dir + decay_rate * param)
        for ref, value in zip(outs[4 * group:4 * group + 4], (new_param, new_mom, new_var, new_param)):
            ref[rows, :] = value.astype(ref.dtype)

    @pl.when(pl.program_id(0) == 0)
    def _():
        update(2, slice(0, ins[8].shape[0]), 0.0)
        for r in range(0, ins[4].shape[0], 8):
            update(1, slice(r, r + 8), WEIGHT_DECAY)

    def rows_of(r, carry):
        update(0, pl.ds(pl.multiple_of(r * 8, 8), 8), WEIGHT_DECAY)
        return carry

    lax.fori_loop(0, ins[0].shape[0] // 8, rows_of, 0)


def solution(mesh):
    dev_count = mesh.shape["dp"] * mesh.shape["fsdp"]

    def local_step(emb_grad, mat_grad, norm_grad, emb_param, emb_mom, emb_var, mat_param, mat_mom, mat_var, norm_param, norm_mom, norm_var):
        width = emb_grad.shape[3]
        emb_rows, mat_rows = emb_param.shape[0], mat_param.shape[0]
        count, shard = norm_param.shape
        emb_in = emb_grad.reshape(2, 2, 2, emb_rows, width)
        mat_in = mat_grad.reshape(2, 2, 2, mat_rows, width)
        norm_in = norm_grad.reshape(count, 1, norm_grad.shape[3])
        rows = emb_rows + mat_rows
        main_rows = rows - 8 * LINE_BLOCKS
        rounds = main_rows // 8 * SPLIT
        half = width // 2
        lines = LINE_BLOCKS * LINE_SPLIT
        quarter = width // LINE_SPLIT // 4
        any_spec = pl.BlockSpec(memory_space=pl.ANY)
        vmem_spec = pl.BlockSpec(memory_space=pltpu.VMEM)
        dma = pltpu.SemaphoreType.DMA
        vmem = lambda *shape: pltpu.VMEM(shape, F32)
        emb_mean, mat_mean, norm_mean, scale = pl.pallas_call(
            functools.partial(reduce_kernel, 1.0 / dev_count),
            out_shape=(
                jax.ShapeDtypeStruct((emb_rows, width), F32),
                jax.ShapeDtypeStruct((mat_rows, width), F32),
                jax.ShapeDtypeStruct((count, shard), F32),
                jax.ShapeDtypeStruct((8, LANES), F32),
            ),
            in_specs=[any_spec] * 3,
            out_specs=(any_spec, any_spec, vmem_spec, vmem_spec),
            scratch_shapes=[
                vmem(2, 2, rows, width),
                vmem(SLOTS, 2, 2, 2, 8, half // SPLIT),
                vmem(2, 2, main_rows, half),
                vmem(2, main_rows, half),
                vmem(rows, width),
                vmem(main_rows, width),
                vmem(lines, 2, 2, 8, 4 * quarter),
                vmem(lines, 2, 2, 8, 3 * quarter),
                vmem(lines, 2, 2, 8, 2 * quarter),
                vmem(lines, 2, 2, 8, quarter),
                vmem(lines, 2, 8, quarter),
                vmem(lines, 8, quarter),
                vmem(*norm_in.shape),
                vmem(2, 2, count, 1, shard),
                vmem(2, 2, count, 1, shard),
                vmem(2, 2, count, 1, shard),
                vmem(2, count, 1, shard),
                vmem(count, 1, shard),
                vmem(count, 1, shard),
                vmem(count, 1, shard),
                vmem(8, LANES),
                vmem(8, LANES),
                vmem(9, 8, LANES),
                dma, dma((rounds,)), dma((SLOTS,)),
                dma((2,)), dma((2, rounds)), dma((2,)), dma((2, rounds)),
                dma, dma((rounds,)), dma, dma((rounds,)), dma,
                dma, dma,
                dma((lines,)), dma((9,)), dma((9, lines)),
                dma, dma((6,)), dma((6,)), dma, dma,
            ],
            compiler_params=pltpu.CompilerParams(collective_id=0, has_side_effects=True, vmem_limit_bytes=VMEM_MIB << 20),
            name="reduce_gradients",
        )(emb_in, mat_in, norm_in)
        block = pl.BlockSpec((ADAM_ROWS, width), lambda i: (i, 0))
        whole_mat = pl.BlockSpec((mat_rows, width), lambda i: (0, 0))
        whole_norm = pl.BlockSpec((count, shard), lambda i: (0, 0))
        specs = [block] * 4 + [whole_mat] * 4 + [whole_norm] * 4
        shapes = []
        for like in (emb_param, mat_param, norm_param):
            shapes += [jax.ShapeDtypeStruct(like.shape, F32)] * 3 + [jax.ShapeDtypeStruct(like.shape, jnp.bfloat16)]
        return pl.pallas_call(
            adam_kernel,
            grid=(emb_rows // ADAM_ROWS,),
            out_shape=tuple(shapes),
            in_specs=[pl.BlockSpec((8, LANES), lambda i: (0, 0))] + specs,
            out_specs=tuple(specs),
            compiler_params=pltpu.CompilerParams(vmem_limit_bytes=24 << 20),
            name="adam",
        )(scale, emb_mean, emb_param, emb_mom, emb_var, mat_mean, mat_param, mat_mom, mat_var,
          norm_mean, norm_param, norm_mom, norm_var)

    grad_spec = P("dp", "fsdp", None, None)
    row_spec = P("fsdp", None)
    col_spec = P(None, "fsdp")
    in_list = (grad_spec, grad_spec, grad_spec, row_spec, row_spec, row_spec, row_spec, row_spec, row_spec, col_spec, col_spec, col_spec)
    out_list = (row_spec, row_spec, row_spec, row_spec, row_spec, row_spec, row_spec, row_spec, col_spec, col_spec, col_spec, col_spec)
    return jax.shard_map(local_step, mesh=mesh, in_specs=in_list, out_specs=out_list, check_vma=False)
```

time: 557 us -> 195 us (0.35)
  waiting for transfers between devices: 483 us -> 0 us
  Pallas kernels: 0 us -> 189 us
  blocking collectives: 34.2 us -> 0 us
  other arithmetic: 20.5 us -> 0 us
  between operations: 16.5 us -> 0.77 us
    reduce_scatter x2 -> x0, waiting for transfers between devices: 274 us -> none  [the longest x1 228 us: local_step(): lax.psum_scatter(emb_grad[0, 0], 'fsdp', scatter_dimension=0, tiled=True)]
    pallas_call x0 -> x2, Pallas kernels: none -> 189 us  [the longest x1 178 us: local_step(): pl.pallas_call(functools.partial(reduce_kernel, 1.0 / dev_count), out_sha...]
    psum x1 -> x0, waiting for transfers between devices: 161 us -> none  [local_step(): emb_mean = lax.psum(emb_part, 'dp') / dev_count]
    unnamed x5 -> x0, waiting for transfers between devices: 47.5 us -> none
    psum x2 -> x0, blocking collectives: 34.2 us -> none  [the longest x1 20.4 us: local_step(): norm_mean = lax.psum(norm_part, 'dp') / dev_count]
    convert_element_type x3 -> x0, other arithmetic: 15 us -> none  [adamw_update(): return (new_param, new_mom, new_var, new_param.astype(jnp.bfloat16))]
  transfers between devices with their start and end apart: 4 -> 0, of which waited for: 4 -> 0; matrix products, arithmetic and copies ran while one was open for 1% -> 0% of each run, Pallas kernels for 0% -> 0%
where the time goes in v3:
time: 195 us
  Pallas kernels  189 us (97%)
  local copies, waits for them, and re-layouts  5.61 us (3%)
    pallas_call x1, Pallas kernels, local_step(): pl.pallas_call(functools.partial(reduce_kernel, 1.0 / dev_count), out_sha...  178 us
    pallas_call x1, Pallas kernels, local_step(): pl.pallas_call(adam_kernel, grid=(emb_rows // ADAM_ROWS,), out_shape=tupl...  10.5 us
    unnamed x22, local copies, waits for them, and re-layouts  5.61 us

profile of v3, /device:TPU:0, one launch (start us, length us, event | category | flops | bytes accessed | tf_op | source)
XLA Modules:
  0.0 195.1 jit_solution(13961296804246443307)
XLA Ops:
  0.6 0.0 copy-start.7
  0.7 0.9 copy-done.7
  1.6 0.0 copy-start
  1.6 0.0 copy-start.1
  1.6 0.0 copy-start.4
  1.6 0.0 copy-start.5
  1.6 0.0 copy-start.6
  1.6 0.0 copy-start.8
  1.6 0.0 copy-start.9
  1.6 0.0 copy-start.10
  1.6 178.2 %reduce_gradients.1 = (f32[256,4608]{1,0:T(8,128)}, f32[16,4608]{1,0:T(8,128)S(1)}, f32[9,576]{1,0:T(8,128)S(1)}, f32[8,128]{1,0:T(8,128)S(1)}) custom-call(f32[2,2,2,256,4608]{4,3,2,1,0:T(8,128)} %bitcast.4, f32[2,2,2,16,4608]{4,3,2,1,0:T(8,128)} %bitcast.5, f32[9,1,4608]{2,1,0:T(1,128)S(1)} %bitcast.3), custom_call_target="tpu_custom_call" | custom-call | tf_op jit(solution)/shard_map/reduce_gradients/pallas_call | solution.py:569
  179.9 0.0 copy-done
  179.9 0.0 copy-done.1
  179.9 0.0 copy-done.4
  179.9 0.0 copy-done.5
  179.9 0.0 copy-done.6
  179.9 0.0 copy-done.8
  179.9 0.0 copy-done.9
  179.9 0.0 copy-done.10
  179.9 0.0 copy-start.2
  180.0 2.3 %copy-done.2 = f32[256,4608]{1,0:T(8,128)S(1)} copy-done((f32[256,4608]{1,0:T(8,128)S(1)}, f32[256,4608]{1,0:T(8,128)}, u32[]{:S(2)}) %copy-start.2) | copy-done | bytes 4718616
  182.3 0.0 copy-start.3
  182.3 2.3 %copy-done.3 = f32[256,4608]{1,0:T(8,128)S(1)} copy-done((f32[256,4608]{1,0:T(8,128)S(1)}, f32[256,4608]{1,0:T(8,128)}, u32[]{:S(2)}) %copy-start.3) | copy-done | bytes 4718616
  184.6 10.5 %adam.1 = (f32[256,4608]{1,0:T(8,128)}, f32[256,4608]{1,0:T(8,128)}, f32[256,4608]{1,0:T(8,128)}, bf16[256,4608]{1,0:T(8,128)(2,1)}, f32[16,4608]{1,0:T(8,128)},...) custom-call(f32[8,128]{1,0:T(8,128)S(1)} %get-tuple-element.16.scale, ...), custom_call_target="tpu_custom_call" | custom-call | tf_op jit(solution)/shard_map/adam/pallas_call | solution.py:620
Async XLA Ops:
  0.6 0.9 copy-start.7
  1.6 178.3 %copy-start = (f32[256,4608]{1,0:T(8,128)S(1)}, f32[256,4608]{1,0:T(8,128)}, u32[]{:S(2)}) copy-start(f32[256,4608]{1,0:T(8,128)} %refs_1_.1) | copy-start | bytes 14155780
  1.6 178.3 %copy-start.1 = (f32[256,4608]{1,0:T(8,128)S(1)}, f32[256,4608]{1,0:T(8,128)}, u32[]{:S(2)}) copy-start(f32[256,4608]{1,0:T(8,128)} %refs_2_.1) | copy-start | bytes 14155780
  1.6 178.3 %copy-start.4 = (f32[16,4608]{1,0:T(8,128)S(1)}, f32[16,4608]{1,0:T(8,128)}, u32[]{:S(2)}) copy-start(f32[16,4608]{1,0:T(8,128)} %refs_5_.1) | copy-start | bytes 884740
  1.6 178.3 %copy-start.5 = (f32[16,4608]{1,0:T(8,128)S(1)}, f32[16,4608]{1,0:T(8,128)}, u32[]{:S(2)}) copy-start(f32[16,4608]{1,0:T(8,128)} %refs_6_.1) | copy-start | bytes 884740
  1.6 178.3 %copy-start.6 = (f32[16,4608]{1,0:T(8,128)S(1)}, f32[16,4608]{1,0:T(8,128)}, u32[]{:S(2)}) copy-start(f32[16,4608]{1,0:T(8,128)} %refs_7_.1) | copy-start | bytes 884740
  1.6 178.3 %copy-start.8 = (f32[9,576]{1,0:T(8,128)S(1)}, f32[9,576]{1,0:T(8,128)}, u32[]{:S(2)}) copy-start(f32[9,576]{1,0:T(8,128)} %refs_9_.1) | copy-start | bytes 62212
  1.6 178.3 %copy-start.9 = (f32[9,576]{1,0:T(8,128)S(1)}, f32[9,576]{1,0:T(8,128)}, u32[]{:S(2)}) copy-start(f32[9,576]{1,0:T(8,128)} %refs_10_.1) | copy-start | bytes 62212
  1.6 178.3 %copy-start.10 = (f32[9,576]{1,0:T(8,128)S(1)}, f32[9,576]{1,0:T(8,128)}, u32[]{:S(2)}) copy-start(f32[9,576]{1,0:T(8,128)} %refs_11_.1) | copy-start | bytes 62212
  179.9 2.3 %copy-start.2 = (f32[256,4608]{1,0:T(8,128)S(1)}, f32[256,4608]{1,0:T(8,128)}, u32[]{:S(2)}) copy-start(f32[256,4608]{1,0:T(8,128)} %refs_3_.1) | copy-start | bytes 14155780
  182.3 2.3 %copy-start.3 = (f32[256,4608]{1,0:T(8,128)S(1)}, f32[256,4608]{1,0:T(8,128)}, u32[]{:S(2)}) copy-start(f32[256,4608]{1,0:T(8,128)} %get-tuple-element.17.refs_0_) | copy-start | bytes 14155780

commit v4 on v3

--- a/solution.py
+++ b/solution.py
@@ -21,22 +21,25 @@
 SPLIT = 2
 AHEAD = 2
 SLOTS = 4
+STATE_ROUND = 16
 CORE_AHEAD = 4
 LAG_ONE, LAG_TWO, LAG_SIDE, LAG_MID, LAG_BACK = 2, 4, 6, 8, 10
-NORM_START, NORM_STEP = 4, 6
+NORM_START, NORM_STEP = 8, 6
 LINE_BLOCKS = 4
 LINE_SPLIT = 3
 LINE_RATE, LINE_STEP = 4, 2
-ADAM_ROWS = 32
-VMEM_MIB = 52
-
-
-def reduce_kernel(inv_count, emb_ref, mat_ref, norm_ref, emb_out, mat_out, norm_out, scale_out,
-                  acc, own, one, two, zin, zmid, lown, lside, lmid, lback, lone, ltwo,
-                  norm_all, nsend, nown, nacc, none, ntwo, nzin, nzmid, sq_main, sq_line, sq_all,
-                  core_send, core_recv, own_sem, one_send, one_recv, two_send, two_recv,
-                  side_send, side_recv, mid_send, mid_recv, back_send, emb_sem, mat_sem,
-                  lown_sem, line_send, line_recv, norm_sem, nsend_sem, nrecv_sem, sq_send, sq_recv):
+ADAM_ROWS, ADAM_COLS = 16, 512
+VMEM_KIB, ADAM_MIB = 45568, 20
+
+
+def reduce_kernel(inv_count, emb_ref, mat_ref, norm_ref, *refs):
+    emb_state, mat_state, state_out = refs[0:3], refs[3:6], refs[9:12]
+    mean_out, norm_out, scale_out = refs[6:9]
+    (acc, own, one, two, zmid, lown, lside, lmid, lback, lone, ltwo,
+     norm_all, nsend, nown, nacc, none, ntwo, nzin, nzmid, sq_main, sq_line, sq_all,
+     core_send, core_recv, own_sem, one_send, one_recv, two_send, two_recv,
+     side_send, side_recv, mid_send, mid_recv, back_send,
+     lown_sem, line_send, line_recv, norm_sem, nsend_sem, nrecv_sem, sq_send, sq_recv, scale_send, scale_recv, state_sem) = refs[12:]
     z = lax.axis_index("dp")
     f = lax.axis_index("fsdp")
     y, x, c = f // 4, (f // 2) % 2, f % 2
@@ -46,7 +49,7 @@
     emb_blocks = emb_ref.shape[3] // 8
     rounds = one.shape[2] // 8 * SPLIT
     emb_rounds = (emb_blocks - LINE_BLOCKS) * SPLIT
-    lines = lown.shape[0]
+    lines = lside.shape[0]
     lwidth = width // LINE_SPLIT
     quarter = lwidth // 4
     is_end = (z == 0) | (z == 3)
@@ -104,7 +107,8 @@
 
     def load_line(i):
         rows, cs = line_at(i)
-        return pltpu.make_async_copy(emb_ref.at[:, :, c, rows, cs], lown.at[i], lown_sem.at[i])
+        slot = lax.rem(i, SLOTS)
+        return pltpu.make_async_copy(emb_ref.at[:, :, c, rows, cs], lown.at[slot], lown_sem.at[slot])
 
     def line_core(i):
         rows, cs = line_at(i)
@@ -114,37 +118,29 @@
     norm_load.start()
     for q in range(AHEAD):
         load_own(jnp.int32(q))
-    for i in range(lines):
-        load_line(jnp.int32(i)).start()
+    load_line(jnp.int32(0)).start()
 
     barrier = pltpu.get_barrier_semaphore()
-    for step in range(1, 8):
-        pl.semaphore_signal(barrier, inc=1, device_id=(z, lax.rem(f + step, 8)), device_id_type=MESH)
     pl.semaphore_signal(barrier, inc=1, device_id=side_peer, device_id_type=MESH)
 
     @pl.when(is_mid)
     def _():
+        for step in range(1, 8):
+            pl.semaphore_signal(barrier, inc=1, device_id=(z, lax.rem(f + step, 8)), device_id_type=MESH)
         pl.semaphore_signal(barrier, inc=1, device_id=mid_peer, device_id_type=MESH)
         pl.semaphore_wait(barrier, 9)
 
     @pl.when(is_end)
     def _():
-        pl.semaphore_wait(barrier, 8)
+        for peer in (core_peer, x_peer, y_peer):
+            pl.semaphore_signal(barrier, inc=1, device_id=peer, device_id_type=MESH)
+        pl.semaphore_wait(barrier, 4)
 
     for q in range(CORE_AHEAD):
-        if q % LINE_RATE == 0:
-            line_core(jnp.int32(q // LINE_RATE)).start()
         send_core(jnp.int32(q))
-
-    norm_load.wait()
-    shard = nacc.shape[4]
-    for yy in range(2):
-        for xx in range(2):
-            at = (4 * yy + 2 * xx) * shard
-            first = norm_all[:, :, at:at + shard]
-            second = norm_all[:, :, at + shard:at + 2 * shard]
-            nsend[yy, xx] = jnp.where(c == 0, second, first)
-            nown[yy, xx] = jnp.where(c == 0, first, second)
+        if q == 0:
+            line_core(jnp.int32(0)).start()
+
     sq_main[...] = jnp.zeros_like(sq_main)
     sq_line[...] = jnp.zeros_like(sq_line)
 
@@ -158,37 +154,17 @@
         src = acc.at[1 - y, x, rb, wide[0]] if h == 0 else acc.at[y, 1 - x, rb, wide[1]]
         return remote(src, two.at[h, inner, cs], two_send.at[h], two_recv.at[h, q], (y_peer, x_peer)[h])
 
-    def side_start(q):
+    def side_copy(q, h):
         rb, _, wide, _ = piece(q)
-        for cs in wide:
-            remote(acc.at[y, x, rb, cs], zin.at[rb, cs], side_send, side_recv.at[q], side_peer).start()
-
-    def mid_start(q):
+        return remote(acc.at[y, x, rb, wide[h]], mean_out.at[rb, wide[h]], side_send, side_recv.at[h, q], side_peer)
+
+    def mid_copy(q, h):
         rb, inner, wide, _ = piece(q)
-        for cs in wide:
-            remote(acc.at[y, x, rb, cs], zmid.at[inner, cs], mid_send, mid_recv.at[q], mid_peer).start()
-
-    def back_start(q):
+        return remote(acc.at[y, x, rb, wide[h]], zmid.at[inner, wide[h]], mid_send, mid_recv.at[h, q], mid_peer)
+
+    def back_copy(q, h):
         rb, _, wide, _ = piece(q)
-        for cs in wide:
-            remote(zin.at[rb, cs], zin.at[rb, cs], back_send, side_recv.at[q], side_peer).start()
-
-    def both(q):
-        _, inner, _, cs = piece(q)
-        return two.at[:, inner, cs]
-
-    def store_out(q):
-        rb, _, wide, _ = piece(q)
-
-        @pl.when(q < emb_rounds)
-        def _():
-            for cs in wide:
-                pltpu.make_async_copy(zin.at[rb, cs], emb_out.at[rb, cs], emb_sem).start()
-
-        @pl.when(q >= emb_rounds)
-        def _():
-            for cs in wide:
-                pltpu.make_async_copy(zin.at[rb, cs], mat_out.at[mat_rows(q), cs], mat_sem).start()
+        return remote(mean_out.at[rb, wide[h]], mean_out.at[rb, wide[h]], back_send, side_recv.at[h, q], side_peer)
 
     def add_squares(part_ref, total):
         sq = total * total
@@ -221,20 +197,15 @@
 
     def gather_side(i):
         rows, cs = line_at(i, 3 * high, 1)
-        return remote(zin.at[rows, cs], zin.at[rows, cs], line_send.at[6], line_recv.at[6, i], side_peer)
+        return remote(mean_out.at[rows, cs], mean_out.at[rows, cs], line_send.at[6], line_recv.at[6, i], side_peer)
 
     def gather_mid(i):
         rows, cs = line_at(i, 2 * high, 2)
-        return remote(zin.at[rows, cs], zin.at[rows, cs], line_send.at[7], line_recv.at[7, i], mid_peer)
+        return remote(mean_out.at[rows, cs], mean_out.at[rows, cs], line_send.at[7], line_recv.at[7, i], mid_peer)
 
     def gather_back(i):
         rows, cs = line_at(i, 1 - high, 3)
-        return remote(zin.at[rows, cs], zin.at[rows, cs], line_send.at[8], line_recv.at[8, i], side_peer)
-
-    def line_out(i):
-        rows, cs = line_at(i)
-        pltpu.make_async_copy(zin.at[rows, cs], emb_out.at[rows, cs], emb_sem).start()
-        add_squares(sq_line, zin[rows, cs])
+        return remote(mean_out.at[rows, cs], mean_out.at[rows, cs], line_send.at[8], line_recv.at[8, i], side_peer)
 
     def either_way(i, do):
         @pl.when(lax.rem(i, 2) == 0)
@@ -248,8 +219,9 @@
     def line_stage_0(i):
         rows, cs = line_at(i)
         load_line(i).wait()
-        take(lown.at[i], line_recv.at[0, i])
-        acc[:, :, rows, cs] = acc[:, :, rows, cs] + lown[i]
+        slot = lax.rem(i, SLOTS)
+        take(lown.at[slot], line_recv.at[0, i])
+        acc[:, :, rows, cs] = acc[:, :, rows, cs] + lown[slot]
 
         @pl.when(is_end)
         def _():
@@ -296,7 +268,7 @@
     def line_stage_5(i):
         rows, cs = line_at(i, z, 1)
         take(ltwo.at[i], line_recv.at[5, i])
-        zin[rows, cs] = (acc[y, x, rows, cs] + ltwo[i]) * inv_count
+        mean_out[rows, cs] = (acc[y, x, rows, cs] + ltwo[i]) * inv_count
 
         @pl.when(is_end)
         def _():
@@ -313,13 +285,13 @@
         def _():
             take(lone.at[i], line_recv.at[7, i])
             gather_back(i).start()
-            line_out(i)
+            rows, cs = line_at(i)
+            add_squares(sq_line, mean_out[rows, cs])
 
     def line_stage_8(i):
         @pl.when(is_end)
         def _():
             take(lside.at[i, 0, 0], line_recv.at[8, i])
-            line_out(i)
 
     line_stages = (line_stage_0, line_stage_1, line_stage_2, line_stage_3, line_stage_4, line_stage_5, line_stage_6,
                    line_stage_7, line_stage_8)
@@ -330,7 +302,10 @@
     norm_side = remote(nacc.at[y, x], nzin, nsend_sem.at[3], nrecv_sem.at[3], side_peer)
     norm_mid = remote(nacc.at[y, x], nzmid, nsend_sem.at[4], nrecv_sem.at[4], mid_peer)
     norm_back = remote(nzin, nzin, nsend_sem.at[5], nrecv_sem.at[3], side_peer)
-    norm_core.start()
+    def state_parts(j):
+        split = emb_state[j].shape[0]
+        return ((emb_state[j], state_out[j].at[pl.ds(0, split)]),
+                (mat_state[j], state_out[j].at[pl.ds(split, mat_state[j].shape[0])]))
 
     def body(t, carry):
         @pl.when(t + CORE_AHEAD < rounds)
@@ -346,6 +321,7 @@
         @pl.when((lax.rem(early, LINE_RATE) == 0) & (early < lines * LINE_RATE))
         def _():
             line_core(lax.div(early, LINE_RATE)).start()
+            load_line(lax.div(early, LINE_RATE)).start()
 
         @pl.when(t < rounds)
         def _():
@@ -378,42 +354,38 @@
                 two_copy(q2, h).wait_recv()
                 acc[y, x, rb, wide[h]] = acc[y, x, rb, wide[h]] + two[h, inner, cs]
 
-            @pl.when(is_end)
-            def _():
-                side_start(q2)
+                @pl.when(is_end)
+                def _(h=h):
+                    side_copy(q2, h).start()
 
         q3 = t - LAG_SIDE
 
         @pl.when(is_mid & (q3 >= 0) & (q3 < rounds))
         def _():
             rb, _, wide, _ = piece(q3)
-            take(both(q3), side_recv.at[q3])
-            for cs in wide:
-                acc[y, x, rb, cs] = acc[y, x, rb, cs] + zin[rb, cs]
-            mid_start(q3)
+            for h in range(2):
+                side_copy(q3, h).wait_recv()
+                acc[y, x, rb, wide[h]] = acc[y, x, rb, wide[h]] + mean_out[rb, wide[h]]
+                mid_copy(q3, h).start()
 
         q4 = t - LAG_MID
 
         @pl.when(is_mid & (q4 >= 0) & (q4 < rounds))
         def _():
             rb, inner, wide, _ = piece(q4)
-            take(both(q4), mid_recv.at[q4])
-            for cs in wide:
-                total = (acc[y, x, rb, cs] + zmid[inner, cs]) * inv_count
-                zin[rb, cs] = total
+            for h in range(2):
+                mid_copy(q4, h).wait_recv()
+                total = (acc[y, x, rb, wide[h]] + zmid[inner, wide[h]]) * inv_count
+                mean_out[rb, wide[h]] = total
+                back_copy(q4, h).start()
                 add_squares(sq_main, total)
-            back_start(q4)
-            store_out(q4)
 
         q5 = t - LAG_BACK
 
         @pl.when(is_end & (q5 >= 0) & (q5 < rounds))
         def _():
-            rb, _, wide, _ = piece(q5)
-            take(both(q5), side_recv.at[q5])
-            store_out(q5)
-            for cs in wide:
-                add_squares(sq_main, zin[rb, cs])
+            for h in range(2):
+                back_copy(q5, h).wait_recv()
 
         for k, stage in enumerate(line_stages):
             late = t - k * LINE_STEP
@@ -421,6 +393,25 @@
             @pl.when((late >= 0) & (late < lines * LINE_RATE) & (lax.rem(late, LINE_RATE) == 0))
             def _(late=late, stage=stage):
                 stage(lax.div(late, LINE_RATE))
+
+        @pl.when(t == STATE_ROUND)
+        def _():
+            for j in range(3):
+                for src, dst in state_parts(j):
+                    pltpu.make_async_copy(src, dst, state_sem.at[j]).start()
+
+        @pl.when(t == NORM_START - NORM_STEP)
+        def _():
+            norm_load.wait()
+            shard = nacc.shape[4]
+            for yy in range(2):
+                for xx in range(2):
+                    at = (4 * yy + 2 * xx) * shard
+                    first = norm_all[:, :, at:at + shard]
+                    second = norm_all[:, :, at + shard:at + 2 * shard]
+                    nsend[yy, xx] = jnp.where(c == 0, second, first)
+                    nown[yy, xx] = jnp.where(c == 0, first, second)
+            norm_core.start()
 
         @pl.when(t == NORM_START)
         def _():
@@ -473,30 +464,39 @@
 
     lax.fori_loop(0, rounds + LAG_BACK, body, 0)
 
-    sq_main[...] = sq_main[...] + sq_line[...] + sq_all[0]
-    for step in range(1, 8):
-        remote(sq_main, sq_all.at[1 + f], sq_send, sq_recv, (z, lax.rem(f + step, 8))).start()
-    sq_all[1 + f] = sq_main[...]
-    seven = sq_all.at[pl.ds(0, 7)]
-    take(seven, sq_recv)
-    square = sq_all[1]
-    for j in range(2, 9):
-        square = square + sq_all[j]
-    scale_out[...] = jnp.minimum(1.0, CLIP_NORM / jnp.sqrt(jnp.broadcast_to(jnp.sum(square), square.shape)))
-
-    take(seven, sq_send)
+    for j in range(3):
+        take(state_out[j], state_sem.at[j])
+    scale_copy = remote(scale_out, scale_out, scale_send, scale_recv, side_peer)
+
+    @pl.when(is_mid)
+    def _():
+        sq_main[...] = sq_main[...] + sq_line[...] + sq_all[0]
+        for step in range(1, 8):
+            remote(sq_main, sq_all.at[1 + f], sq_send, sq_recv, (z, lax.rem(f + step, 8))).start()
+        sq_all[1 + f] = sq_main[...]
+        seven = sq_all.at[pl.ds(0, 7)]
+        take(seven, sq_recv)
+        square = sq_all[1]
+        for j in range(2, 9):
+            square = square + sq_all[j]
+        scale_out[...] = jnp.minimum(1.0, CLIP_NORM / jnp.sqrt(jnp.broadcast_to(jnp.sum(square), square.shape)))
+        scale_copy.start()
+        take(seven, sq_send)
+
+    @pl.when(is_end)
+    def _():
+        scale_copy.wait_recv()
+
     take(acc.at[:, :, pl.ds(0, one.shape[2])], core_send)
     for h in range(2):
         take(one.at[h], one_send.at[h])
         take(two.at[h], two_send.at[h])
-    take(lown, line_send.at[0])
+    take(acc.at[:, :, pl.ds(0, 8 * LINE_BLOCKS)], line_send.at[0])
     take(lone, line_send.at[4])
     take(ltwo, line_send.at[5])
     norm_core.wait_send()
     norm_one.wait_send()
     norm_two.wait_send()
-    take(emb_out, emb_sem)
-    take(mat_out, mat_sem)
 
     @pl.when(is_end)
     def _():
@@ -515,35 +515,43 @@
         take(lside.at[:, 0, 0], line_send.at[8])
         norm_mid.wait_send()
         norm_back.wait_send()
-
-
-def adam_kernel(scale_ref, *refs):
-    ins, outs = refs[:12], refs[12:]
+        scale_copy.wait_send()
+
+
+def adam_kernel(scale_ref, mean_ref, norm_ref, *refs):
+    ins, outs, news, sems = refs[:6], refs[6:18], refs[18:30], refs[30]
     clip = scale_ref[0:1, 0:1]
-    bias_one = 1.0 / (1.0 - BETA_ONE ** ADAM_STEP)
+    rate = LEARN_RATE / (1.0 - BETA_ONE ** ADAM_STEP)
     bias_two = 1.0 / (1.0 - BETA_TWO ** ADAM_STEP)
-
-    def update(group, rows, decay_rate):
-        grad, param, mom, var = (ref[rows, :] for ref in ins[4 * group:4 * group + 4])
-        grad = grad * clip
-        new_mom = BETA_ONE * mom + (1.0 - BETA_ONE) * grad
-        new_var = BETA_TWO * var + (1.0 - BETA_TWO) * grad * grad
-        step_dir = new_mom * bias_one / (jnp.sqrt(new_var * bias_two) + ADAM_EPS)
-        new_param = param - LEARN_RATE * (step_dir + decay_rate * param)
-        for ref, value in zip(outs[4 * group:4 * group + 4], (new_param, new_mom, new_var, new_param)):
-            ref[rows, :] = value.astype(ref.dtype)
-
-    @pl.when(pl.program_id(0) == 0)
-    def _():
-        update(2, slice(0, ins[8].shape[0]), 0.0)
-        for r in range(0, ins[4].shape[0], 8):
-            update(1, slice(r, r + 8), WEIGHT_DECAY)
-
-    def rows_of(r, carry):
-        update(0, pl.ds(pl.multiple_of(r * 8, 8), 8), WEIGHT_DECAY)
+    emb_rows = outs[0].shape[0]
+
+    def update(group, grad_ref, states, source, start, rows, decay_rate):
+        width = grad_ref.shape[1]
+        cols = ADAM_COLS if width % ADAM_COLS == 0 else width
+        at, here = pl.ds(start, rows), pl.ds(source + start, rows)
+        for left in range(0, width, cols):
+            cs = pl.ds(left, cols)
+            grad = grad_ref[here, cs] * clip
+            param, mom, var = (ref[here, cs] for ref in states)
+            new_mom = BETA_ONE * mom + (1.0 - BETA_ONE) * grad
+            new_var = BETA_TWO * var + (1.0 - BETA_TWO) * grad * grad
+            move = rate * new_mom / (jnp.sqrt(new_var * bias_two) + ADAM_EPS)
+            new_param = (1.0 - LEARN_RATE * decay_rate) * param - move
+            for ref, value in zip(news[4 * group:4 * group + 4], (new_param, new_mom, new_var, new_param)):
+                ref[at, cs] = value.astype(ref.dtype)
+        for k in range(4 * group, 4 * group + 4):
+            pltpu.make_async_copy(news[k].at[at], outs[k].at[at], sems.at[k]).start()
+
+    update(2, norm_ref, ins[3:], 0, 0, norm_ref.shape[0], 0.0)
+    update(1, mean_ref, ins[:3], emb_rows, 0, outs[4].shape[0], WEIGHT_DECAY)
+
+    def some_rows(r, carry):
+        update(0, mean_ref, ins[:3], 0, pl.multiple_of(r * ADAM_ROWS, ADAM_ROWS), ADAM_ROWS, WEIGHT_DECAY)
         return carry
 
-    lax.fori_loop(0, ins[0].shape[0] // 8, rows_of, 0)
+    lax.fori_loop(0, emb_rows // ADAM_ROWS, some_rows, 0)
+    for k in range(12):
+        pltpu.make_async_copy(outs[k], outs[k], sems.at[k]).wait()
 
 
 def solution(mesh):
@@ -566,24 +574,22 @@
         vmem_spec = pl.BlockSpec(memory_space=pltpu.VMEM)
         dma = pltpu.SemaphoreType.DMA
         vmem = lambda *shape: pltpu.VMEM(shape, F32)
-        emb_mean, mat_mean, norm_mean, scale = pl.pallas_call(
+        mean, norm_mean, scale, param, mom, var = pl.pallas_call(
             functools.partial(reduce_kernel, 1.0 / dev_count),
             out_shape=(
-                jax.ShapeDtypeStruct((emb_rows, width), F32),
-                jax.ShapeDtypeStruct((mat_rows, width), F32),
-                jax.ShapeDtypeStruct((count, shard), F32),
-                jax.ShapeDtypeStruct((8, LANES), F32),
-            ),
-            in_specs=[any_spec] * 3,
-            out_specs=(any_spec, any_spec, vmem_spec, vmem_spec),
+                vmem(rows, width),
+                vmem(count, shard),
+                vmem(8, LANES),
+            ) + (vmem(rows, width),) * 3,
+            in_specs=[any_spec] * 9,
+            out_specs=(vmem_spec,) * 6,
             scratch_shapes=[
                 vmem(2, 2, rows, width),
                 vmem(SLOTS, 2, 2, 2, 8, half // SPLIT),
                 vmem(2, 2, main_rows, half),
                 vmem(2, main_rows, half),
-                vmem(rows, width),
                 vmem(main_rows, width),
-                vmem(lines, 2, 2, 8, 4 * quarter),
+                vmem(SLOTS, 2, 2, 8, 4 * quarter),
                 vmem(lines, 2, 2, 8, 3 * quarter),
                 vmem(lines, 2, 2, 8, 2 * quarter),
                 vmem(lines, 2, 2, 8, quarter),
@@ -602,31 +608,26 @@
                 vmem(9, 8, LANES),
                 dma, dma((rounds,)), dma((SLOTS,)),
                 dma((2,)), dma((2, rounds)), dma((2,)), dma((2, rounds)),
-                dma, dma((rounds,)), dma, dma((rounds,)), dma,
-                dma, dma,
-                dma((lines,)), dma((9,)), dma((9, lines)),
-                dma, dma((6,)), dma((6,)), dma, dma,
+                dma, dma((2, rounds)), dma, dma((2, rounds)), dma,
+                dma((SLOTS,)), dma((9,)), dma((9, lines)),
+                dma, dma((6,)), dma((6,)), dma, dma, dma, dma, dma((3,)),
             ],
-            compiler_params=pltpu.CompilerParams(collective_id=0, has_side_effects=True, vmem_limit_bytes=VMEM_MIB << 20),
+            compiler_params=pltpu.CompilerParams(collective_id=0, has_side_effects=True, vmem_limit_bytes=VMEM_KIB << 10),
             name="reduce_gradients",
-        )(emb_in, mat_in, norm_in)
-        block = pl.BlockSpec((ADAM_ROWS, width), lambda i: (i, 0))
-        whole_mat = pl.BlockSpec((mat_rows, width), lambda i: (0, 0))
-        whole_norm = pl.BlockSpec((count, shard), lambda i: (0, 0))
-        specs = [block] * 4 + [whole_mat] * 4 + [whole_norm] * 4
+        )(*(pltpu.with_memory_space_constraint(a, pltpu.HBM) for a in (
+            emb_in, mat_in, norm_in, emb_param, emb_mom, emb_var, mat_param, mat_mom, mat_var)))
         shapes = []
         for like in (emb_param, mat_param, norm_param):
             shapes += [jax.ShapeDtypeStruct(like.shape, F32)] * 3 + [jax.ShapeDtypeStruct(like.shape, jnp.bfloat16)]
         return pl.pallas_call(
             adam_kernel,
-            grid=(emb_rows // ADAM_ROWS,),
             out_shape=tuple(shapes),
-            in_specs=[pl.BlockSpec((8, LANES), lambda i: (0, 0))] + specs,
-            out_specs=tuple(specs),
-            compiler_params=pltpu.CompilerParams(vmem_limit_bytes=24 << 20),
+            in_specs=[vmem_spec] * 9,
+            out_specs=(any_spec,) * 12,
+            scratch_shapes=[pltpu.VMEM(like.shape, like.dtype) for like in shapes] + [dma((12,))],
+            compiler_params=pltpu.CompilerParams(vmem_limit_bytes=ADAM_MIB << 20),
             name="adam",
-        )(scale, emb_mean, emb_param, emb_mom, emb_var, mat_mean, mat_param, mat_mom, mat_var,
-          norm_mean, norm_param, norm_mom, norm_var)
+        )(scale, mean, norm_mean, param, mom, var, norm_param, norm_mom, norm_var)
 
     grad_spec = P("dp", "fsdp", None, None)
     row_spec = P("fsdp", None)

time: 195 us -> 185 us (0.949)
  local copies, waits for them, and re-layouts: 5.61 us -> 0.01 us
  Pallas kernels: 189 us -> 184 us
    unnamed x22 -> x6, local copies, waits for them, and re-layouts: 5.61 us -> 0.01 us
    pallas_call x1, Pallas kernels: 10.5 us -> 6.46 us  [local_step(): pl.pallas_call(adam_kernel, out_shape=tuple(shapes), in_specs=[vmem_spec]...]
where the time goes in v4:
time: 185 us
  Pallas kernels  184 us (99%)
    pallas_call x1, Pallas kernels, local_step(): pl.pallas_call(functools.partial(reduce_kernel, 1.0 / dev_count), out_sha...  177 us
    pallas_call x1, Pallas kernels, local_step(): pl.pallas_call(adam_kernel, out_shape=tuple(shapes), in_specs=[vmem_spec]...  6.46 us

profile of v4, /device:TPU:0, one launch (start us, length us, event | category | flops | bytes accessed | tf_op | source)
XLA Modules:
  0.0 184.6 jit_solution(11356022702398970094)
XLA Ops:
  0.6 0.0 copy-start
  0.7 0.0 copy-start.1
  0.7 0.0 copy-start.2
  0.7 177.5 %reduce_gradients.1 = (f32[272,4608]{1,0:T(8,128)S(1)}, f32[9,576]{1,0:T(8,128)S(1)}, f32[8,128]{1,0:T(8,128)S(1)}, f32[272,4608]{1,0:T(8,128)S(1)}, f32[272,4608]{1,0:T(8,128)S(1)}, /*index=5*/f32[272,4608]{1,0:T(8,128)S(1)}) custom-call(f32[2,2,2,256,4608]{4,3,2,1,0:T(8,128)} %bitcast.3, f32[2,2,2,16,4608]{4,3,2,1,0:T(8,128)} %bitcast.4, ...), custom_call_target="tpu_custom_call" | custom-call | tf_op jit(solution)/shard_map/reduce_gradients/pallas_call | solution.py:577
  178.1 0.0 copy-done
  178.2 0.0 copy-done.1
  178.2 0.0 copy-done.2
  178.2 6.5 %adam.1 = (f32[256,4608]{1,0:T(8,128)}, f32[256,4608]{1,0:T(8,128)}, f32[256,4608]{1,0:T(8,128)}, bf16[256,4608]{1,0:T(8,128)(2,1)}, f32[16,4608]{1,0:T(8,128)},...) custom-call(f32[8,128]{1,0:T(8,128)S(1)} %get-tuple-element.18.scale, ...), custom_call_target="tpu_custom_call" | custom-call | tf_op jit(solution)/shard_map/adam/pallas_call | solution.py:622
Async XLA Ops:
  0.6 177.5 %copy-start = (f32[9,576]{1,0:T(8,128)S(1)}, f32[9,576]{1,0:T(8,128)}, u32[]{:S(2)}) copy-start(f32[9,576]{1,0:T(8,128)} %refs_3_.3) | copy-start | bytes 62212
  0.7 177.5 %copy-start.1 = (f32[9,576]{1,0:T(8,128)S(1)}, f32[9,576]{1,0:T(8,128)}, u32[]{:S(2)}) copy-start(f32[9,576]{1,0:T(8,128)} %refs_4_.3) | copy-start | bytes 62212
  0.7 177.5 %copy-start.2 = (f32[9,576]{1,0:T(8,128)S(1)}, f32[9,576]{1,0:T(8,128)}, u32[]{:S(2)}) copy-start(f32[9,576]{1,0:T(8,128)} %refs_5_.3) | copy-start | bytes 62212

commit v5 on v4

--- a/solution.py
+++ b/solution.py
@@ -21,6 +21,7 @@
 SPLIT = 2
 AHEAD = 2
 SLOTS = 4
+CORE_RING, RING, LINE_RING = 12, 8, 4
 STATE_ROUND = 16
 CORE_AHEAD = 4
 LAG_ONE, LAG_TWO, LAG_SIDE, LAG_MID, LAG_BACK = 2, 4, 6, 8, 10
@@ -68,6 +69,12 @@
     def take(ref, sem):
         pltpu.make_async_copy(ref, ref, sem).wait()
 
+    def ring(q):
+        return lax.rem(q, RING)
+
+    def line_ring(i):
+        return lax.rem(i, LINE_RING)
+
     def piece(q):
         block, sub = lax.div(q, SPLIT), lax.rem(q, SPLIT) * cols
         rows = pl.ds(pl.multiple_of((block + LINE_BLOCKS) * 8, 8), 8)
@@ -99,7 +106,7 @@
     def send_core(q):
         rb = piece(q)[0]
         from_emb_or_mat(q, lambda ref, rows, h, cs: remote(
-            ref.at[:, :, 1 - c, rows, cs], acc.at[:, :, rb, cs], core_send, core_recv.at[q], core_peer).start())
+            ref.at[:, :, 1 - c, rows, cs], acc.at[:, :, rb, cs], core_send, core_recv.at[lax.rem(q, CORE_RING)], core_peer).start())
 
     def line_at(i, start=0, size=4):
         rows = pl.ds(pl.multiple_of(lax.div(i, LINE_SPLIT) * 8, 8), 8)
@@ -112,7 +119,7 @@
 
     def line_core(i):
         rows, cs = line_at(i)
-        return remote(emb_ref.at[:, :, 1 - c, rows, cs], acc.at[:, :, rows, cs], line_send.at[0], line_recv.at[0, i], core_peer)
+        return remote(emb_ref.at[:, :, 1 - c, rows, cs], acc.at[:, :, rows, cs], line_send.at[0], line_recv.at[0, line_ring(i)], core_peer)
 
     norm_load = pltpu.make_async_copy(norm_ref, norm_all, norm_sem)
     norm_load.start()
@@ -147,24 +154,24 @@
     def one_copy(q, h):
         rb, inner, wide, cs = piece(q)
         src = acc.at[:, 1 - x, rb, wide[0]] if h == 0 else acc.at[1 - y, :, rb, wide[1]]
-        return remote(src, one.at[h, :, inner, cs], one_send.at[h], one_recv.at[h, q], (x_peer, y_peer)[h])
+        return remote(src, one.at[h, :, inner, cs], one_send.at[h], one_recv.at[h, ring(q)], (x_peer, y_peer)[h])
 
     def two_copy(q, h):
         rb, inner, wide, cs = piece(q)
         src = acc.at[1 - y, x, rb, wide[0]] if h == 0 else acc.at[y, 1 - x, rb, wide[1]]
-        return remote(src, two.at[h, inner, cs], two_send.at[h], two_recv.at[h, q], (y_peer, x_peer)[h])
+        return remote(src, two.at[h, inner, cs], two_send.at[h], two_recv.at[h, ring(q)], (y_peer, x_peer)[h])
 
     def side_copy(q, h):
         rb, _, wide, _ = piece(q)
-        return remote(acc.at[y, x, rb, wide[h]], mean_out.at[rb, wide[h]], side_send, side_recv.at[h, q], side_peer)
+        return remote(acc.at[y, x, rb, wide[h]], mean_out.at[rb, wide[h]], side_send, side_recv.at[h, ring(q)], side_peer)
 
     def mid_copy(q, h):
         rb, inner, wide, _ = piece(q)
-        return remote(acc.at[y, x, rb, wide[h]], zmid.at[inner, wide[h]], mid_send, mid_recv.at[h, q], mid_peer)
+        return remote(acc.at[y, x, rb, wide[h]], zmid.at[inner, wide[h]], mid_send, mid_recv.at[h, ring(q)], mid_peer)
 
     def back_copy(q, h):
         rb, _, wide, _ = piece(q)
-        return remote(mean_out.at[rb, wide[h]], mean_out.at[rb, wide[h]], back_send, side_recv.at[h, q], side_peer)
+        return remote(mean_out.at[rb, wide[h]], mean_out.at[rb, wide[h]], back_send, side_recv.at[h, ring(q)], side_peer)
 
     def add_squares(part_ref, total):
         sq = total * total
@@ -175,37 +182,37 @@
 
     def line_side(i):
         rows, cs = line_at(i, 1 - high, 3)
-        return remote(acc.at[:, :, rows, cs], lside.at[i], line_send.at[1], line_recv.at[1, i], side_peer)
+        return remote(acc.at[:, :, rows, cs], lside.at[i], line_send.at[1], line_recv.at[1, line_ring(i)], side_peer)
 
     def line_mid(i):
         rows, cs = line_at(i, 2 - 2 * high, 2)
-        return remote(acc.at[:, :, rows, cs], lmid.at[i], line_send.at[2], line_recv.at[2, i], mid_peer)
+        return remote(acc.at[:, :, rows, cs], lmid.at[i], line_send.at[2], line_recv.at[2, line_ring(i)], mid_peer)
 
     def line_back(i):
         rows, cs = line_at(i, 3 * high, 1)
-        return remote(acc.at[:, :, rows, cs], lback.at[i], line_send.at[3], line_recv.at[3, i], side_peer)
+        return remote(acc.at[:, :, rows, cs], lback.at[i], line_send.at[3], line_recv.at[3, line_ring(i)], side_peer)
 
     def line_one(i, h):
         rows, cs = line_at(i, z, 1)
         src = acc.at[:, 1 - x, rows, cs] if h == 0 else acc.at[1 - y, :, rows, cs]
-        return remote(src, lone.at[i], line_send.at[4], line_recv.at[4, i], (x_peer, y_peer)[h])
+        return remote(src, lone.at[i], line_send.at[4], line_recv.at[4, line_ring(i)], (x_peer, y_peer)[h])
 
     def line_two(i, h):
         rows, cs = line_at(i, z, 1)
         src = acc.at[1 - y, x, rows, cs] if h == 0 else acc.at[y, 1 - x, rows, cs]
-        return remote(src, ltwo.at[i], line_send.at[5], line_recv.at[5, i], (y_peer, x_peer)[h])
+        return remote(src, ltwo.at[i], line_send.at[5], line_recv.at[5, line_ring(i)], (y_peer, x_peer)[h])
 
     def gather_side(i):
         rows, cs = line_at(i, 3 * high, 1)
-        return remote(mean_out.at[rows, cs], mean_out.at[rows, cs], line_send.at[6], line_recv.at[6, i], side_peer)
+        return remote(mean_out.at[rows, cs], mean_out.at[rows, cs], line_send.at[6], line_recv.at[6, line_ring(i)], side_peer)
 
     def gather_mid(i):
         rows, cs = line_at(i, 2 * high, 2)
-        return remote(mean_out.at[rows, cs], mean_out.at[rows, cs], line_send.at[7], line_recv.at[7, i], mid_peer)
+        return remote(mean_out.at[rows, cs], mean_out.at[rows, cs], line_send.at[7], line_recv.at[7, line_ring(i)], mid_peer)
 
     def gather_back(i):
         rows, cs = line_at(i, 1 - high, 3)
-        return remote(mean_out.at[rows, cs], mean_out.at[rows, cs], line_send.at[8], line_recv.at[8, i], side_peer)
+        return remote(mean_out.at[rows, cs], mean_out.at[rows, cs], line_send.at[8], line_recv.at[8, line_ring(i)], side_peer)
 
     def either_way(i, do):
         @pl.when(lax.rem(i, 2) == 0)
@@ -220,7 +227,7 @@
         rows, cs = line_at(i)
         load_line(i).wait()
         slot = lax.rem(i, SLOTS)
-        take(lown.at[slot], line_recv.at[0, i])
+        take(lown.at[slot], line_recv.at[0, line_ring(i)])
         acc[:, :, rows, cs] = acc[:, :, rows, cs] + lown[slot]
 
         @pl.when(is_end)
@@ -231,7 +238,7 @@
         @pl.when(is_mid)
         def _():
             rows, cs = line_at(i, 1 - high, 3)
-            take(lside.at[i], line_recv.at[1, i])
+            take(lside.at[i], line_recv.at[1, line_ring(i)])
             acc[:, :, rows, cs] = acc[:, :, rows, cs] + lside[i]
             line_mid(i).start()
 
@@ -239,7 +246,7 @@
         @pl.when(is_mid)
         def _():
             rows, cs = line_at(i, 2 * high, 2)
-            take(lmid.at[i], line_recv.at[2, i])
+            take(lmid.at[i], line_recv.at[2, line_ring(i)])
             acc[:, :, rows, cs] = acc[:, :, rows, cs] + lmid[i]
             line_back(i).start()
 
@@ -247,14 +254,14 @@
         @pl.when(is_end)
         def _():
             rows, cs = line_at(i, 3 * high, 1)
-            take(lback.at[i], line_recv.at[3, i])
+            take(lback.at[i], line_recv.at[3, line_ring(i)])
             acc[:, :, rows, cs] = acc[:, :, rows, cs] + lback[i]
 
         either_way(i, lambda h: line_one(i, h).start())
 
     def line_stage_4(i):
         rows, cs = line_at(i, z, 1)
-        take(lone.at[i], line_recv.at[4, i])
+        take(lone.at[i], line_recv.at[4, line_ring(i)])
 
         def add(h):
             if h == 0:
@@ -267,7 +274,7 @@
 
     def line_stage_5(i):
         rows, cs = line_at(i, z, 1)
-        take(ltwo.at[i], line_recv.at[5, i])
+        take(ltwo.at[i], line_recv.at[5, line_ring(i)])
         mean_out[rows, cs] = (acc[y, x, rows, cs] + ltwo[i]) * inv_count
 
         @pl.when(is_end)
@@ -277,13 +284,13 @@
     def line_stage_6(i):
         @pl.when(is_mid)
         def _():
-            take(ltwo.at[i], line_recv.at[6, i])
+            take(ltwo.at[i], line_recv.at[6, line_ring(i)])
             gather_mid(i).start()
 
     def line_stage_7(i):
         @pl.when(is_mid)
         def _():
-            take(lone.at[i], line_recv.at[7, i])
+            take(lone.at[i], line_recv.at[7, line_ring(i)])
             gather_back(i).start()
             rows, cs = line_at(i)
             add_squares(sq_line, mean_out[rows, cs])
@@ -291,7 +298,7 @@
     def line_stage_8(i):
         @pl.when(is_end)
         def _():
-            take(lside.at[i, 0, 0], line_recv.at[8, i])
+            take(lside.at[i, 0, 0], line_recv.at[8, line_ring(i)])
 
     line_stages = (line_stage_0, line_stage_1, line_stage_2, line_stage_3, line_stage_4, line_stage_5, line_stage_6,
                    line_stage_7, line_stage_8)
@@ -328,7 +335,7 @@
             rb, _, wide, _ = piece(t)
             slot = lax.rem(t, SLOTS)
             take(own.at[slot], own_sem.at[slot])
-            take(own.at[slot], core_recv.at[t])
+            take(own.at[slot], core_recv.at[lax.rem(t, CORE_RING)])
             for h in range(2):
                 acc[:, :, rb, wide[h]] = acc[:, :, rb, wide[h]] + own[slot, h]
                 one_copy(t, h).start()
@@ -606,10 +613,10 @@
                 vmem(8, LANES),
                 vmem(8, LANES),
                 vmem(9, 8, LANES),
-                dma, dma((rounds,)), dma((SLOTS,)),
-                dma((2,)), dma((2, rounds)), dma((2,)), dma((2, rounds)),
-                dma, dma((2, rounds)), dma, dma((2, rounds)), dma,
-                dma((SLOTS,)), dma((9,)), dma((9, lines)),
+                dma, dma((CORE_RING,)), dma((SLOTS,)),
+                dma((2,)), dma((2, RING)), dma((2,)), dma((2, RING)),
+                dma, dma((2, RING)), dma, dma((2, RING)), dma,
+                dma((SLOTS,)), dma((9,)), dma((9, LINE_RING)),
                 dma, dma((6,)), dma((6,)), dma, dma, dma, dma, dma((3,)),
             ],
             compiler_params=pltpu.CompilerParams(collective_id=0, has_side_effects=True, vmem_limit_bytes=VMEM_KIB << 10),

time: 185 us -> 180 us (0.973)
  Pallas kernels: 184 us -> 179 us
    pallas_call x1, Pallas kernels: 177 us -> 173 us  [local_step(): pl.pallas_call(functools.partial(reduce_kernel, 1.0 / dev_count), out_sha...]
where the time goes in v5:
time: 180 us
  Pallas kernels  179 us (99%)
    pallas_call x1, Pallas kernels, local_step(): pl.pallas_call(functools.partial(reduce_kernel, 1.0 / dev_count), out_sha...  173 us
    pallas_call x1, Pallas kernels, local_step(): pl.pallas_call(adam_kernel, out_shape=tuple(shapes), in_specs=[vmem_spec]...  6.46 us

profile of v5, /device:TPU:0, one launch (start us, length us, event | category | flops | bytes accessed | tf_op | source)
XLA Modules:
  0.0 179.9 jit_solution(2310793043853874991)
XLA Ops:
  0.6 0.0 copy-start
  0.7 0.0 copy-start.1
  0.7 0.0 copy-start.2
  0.7 172.7 %reduce_gradients.1 = (f32[272,4608]{1,0:T(8,128)S(1)}, f32[9,576]{1,0:T(8,128)S(1)}, f32[8,128]{1,0:T(8,128)S(1)}, f32[272,4608]{1,0:T(8,128)S(1)}, f32[272,4608]{1,0:T(8,128)S(1)}, /*index=5*/f32[272,4608]{1,0:T(8,128)S(1)}) custom-call(f32[2,2,2,256,4608]{4,3,2,1,0:T(8,128)} %bitcast.3, f32[2,2,2,16,4608]{4,3,2,1,0:T(8,128)} %bitcast.4, ...), custom_call_target="tpu_custom_call" | custom-call | tf_op jit(solution)/shard_map/reduce_gradients/pallas_call | solution.py:584
  173.4 0.0 copy-done
  173.4 0.0 copy-done.1
  173.4 0.0 copy-done.2
  173.4 6.5 %adam.1 = (f32[256,4608]{1,0:T(8,128)}, f32[256,4608]{1,0:T(8,128)}, f32[256,4608]{1,0:T(8,128)}, bf16[256,4608]{1,0:T(8,128)(2,1)}, f32[16,4608]{1,0:T(8,128)},...) custom-call(f32[8,128]{1,0:T(8,128)S(1)} %get-tuple-element.18.scale, ...), custom_call_target="tpu_custom_call" | custom-call | tf_op jit(solution)/shard_map/adam/pallas_call | solution.py:629
Async XLA Ops:
  0.6 172.7 %copy-start = (f32[9,576]{1,0:T(8,128)S(1)}, f32[9,576]{1,0:T(8,128)}, u32[]{:S(2)}) copy-start(f32[9,576]{1,0:T(8,128)} %refs_3_.3) | copy-start | bytes 62212
  0.7 172.7 %copy-start.1 = (f32[9,576]{1,0:T(8,128)S(1)}, f32[9,576]{1,0:T(8,128)}, u32[]{:S(2)}) copy-start(f32[9,576]{1,0:T(8,128)} %refs_4_.3) | copy-start | bytes 62212
  0.7 172.7 %copy-start.2 = (f32[9,576]{1,0:T(8,128)S(1)}, f32[9,576]{1,0:T(8,128)}, u32[]{:S(2)}) copy-start(f32[9,576]{1,0:T(8,128)} %refs_5_.3) | copy-start | bytes 62212

commit v6 on v5

--- a/solution.py
+++ b/solution.py
@@ -18,17 +18,17 @@
 MESH = pl.DeviceIdType.MESH
 F32 = jnp.float32
 LANES = 128
-SPLIT = 2
+SPLIT = 3
 AHEAD = 2
 SLOTS = 4
-CORE_RING, RING, LINE_RING = 12, 8, 4
+CORE_RING, RING, LINE_RING = 12, 12, 5
 STATE_ROUND = 16
 CORE_AHEAD = 4
-LAG_ONE, LAG_TWO, LAG_SIDE, LAG_MID, LAG_BACK = 2, 4, 6, 8, 10
-NORM_START, NORM_STEP = 8, 6
-LINE_BLOCKS = 4
+LAG_ONE, LAG_TWO, LAG_SIDE, LAG_MID, LAG_BACK = 3, 6, 9, 12, 15
+NORM_START, NORM_STEP = 12, 6
+LINE_BLOCKS = 5
 LINE_SPLIT = 3
-LINE_RATE, LINE_STEP = 4, 2
+LINE_RATE, LINE_STEP = 5, 3
 ADAM_ROWS, ADAM_COLS = 16, 512
 VMEM_KIB, ADAM_MIB = 45568, 20
 

time: 180 us -> 180 us (level)
  no operation moved by 1% of the time
where the time goes in v6:
time: 180 us; the launch traced here: 179 us
  Pallas kernels  179 us (99%)
    pallas_call x1, Pallas kernels, local_step(): pl.pallas_call(functools.partial(reduce_kernel, 1.0 / dev_count), out_sha...  172 us
    pallas_call x1, Pallas kernels, local_step(): pl.pallas_call(adam_kernel, out_shape=tuple(shapes), in_specs=[vmem_spec]...  6.46 us

profile of v6, /device:TPU:0, one launch (start us, length us, event | category | flops | bytes accessed | tf_op | source)
XLA Modules:
  0.0 179.4 jit_solution(9289224362449308686)
XLA Ops:
  0.6 0.0 copy-start
  0.7 0.0 copy-start.1
  0.7 0.0 copy-start.2
  0.7 172.3 %reduce_gradients.1 = (f32[272,4608]{1,0:T(8,128)S(1)}, f32[9,576]{1,0:T(8,128)S(1)}, f32[8,128]{1,0:T(8,128)S(1)}, f32[272,4608]{1,0:T(8,128)S(1)}, f32[272,4608]{1,0:T(8,128)S(1)}, /*index=5*/f32[272,4608]{1,0:T(8,128)S(1)}) custom-call(f32[2,2,2,256,4608]{4,3,2,1,0:T(8,128)} %bitcast.3, f32[2,2,2,16,4608]{4,3,2,1,0:T(8,128)} %bitcast.4, ...), custom_call_target="tpu_custom_call" | custom-call | tf_op jit(solution)/shard_map/reduce_gradients/pallas_call | solution.py:584
  173.0 0.0 copy-done
  173.0 0.0 copy-done.1
  173.0 0.0 copy-done.2
  173.0 6.5 %adam.1 = (f32[256,4608]{1,0:T(8,128)}, f32[256,4608]{1,0:T(8,128)}, f32[256,4608]{1,0:T(8,128)}, bf16[256,4608]{1,0:T(8,128)(2,1)}, f32[16,4608]{1,0:T(8,128)},...) custom-call(f32[8,128]{1,0:T(8,128)S(1)} %get-tuple-element.18.scale, ...), custom_call_target="tpu_custom_call" | custom-call | tf_op jit(solution)/shard_map/adam/pallas_call | solution.py:629
Async XLA Ops:
  0.6 172.3 %copy-start = (f32[9,576]{1,0:T(8,128)S(1)}, f32[9,576]{1,0:T(8,128)}, u32[]{:S(2)}) copy-start(f32[9,576]{1,0:T(8,128)} %refs_3_.3) | copy-start | bytes 62212
  0.7 172.3 %copy-start.1 = (f32[9,576]{1,0:T(8,128)S(1)}, f32[9,576]{1,0:T(8,128)}, u32[]{:S(2)}) copy-start(f32[9,576]{1,0:T(8,128)} %refs_4_.3) | copy-start | bytes 62212
  0.7 172.3 %copy-start.2 = (f32[9,576]{1,0:T(8,128)S(1)}, f32[9,576]{1,0:T(8,128)}, u32[]{:S(2)}) copy-start(f32[9,576]{1,0:T(8,128)} %refs_5_.3) | copy-start | bytes 62212
